TPU v7x, 256 devices: a whole 4x4x8 slice. The times are simulated.
256 devices in a mesh: seq: 32 (over x, z_hi, y), tp: 8 (over z_lo, core).
Axes of the slice: x: 4, y: 4, z: 8 (z_hi: 2, z_lo: 4; z = z_hi * 4 + z_lo), core: 2. Of those that a mesh axis runs over, the one named last changes fastest.
Arguments:
- latent: bfloat16 [2, 32, 1024, 1152], P(None, 'seq', 'tp'), may hold values from -6 to 6
- modulation: float32 [2, 9, 1152], replicated, may hold values from -4 to 4
- qkv_spatial: bfloat16 [3, 1152, 1152], P(None, None, 'tp'), may hold values from -0.1875 to 0.1875
- gain_spatial: float32 [2, 72], replicated, may hold values from 0.5 to 1.7
- out_spatial: bfloat16 [1152, 1152], P('tp'), may hold values from -0.1875 to 0.1875
- qkv_temporal: bfloat16 [3, 1152, 1152], P(None, None, 'tp'), may hold values from -0.1875 to 0.1875
- gain_temporal: float32 [2, 72], replicated, may hold values from 0.5 to 1.7
- out_temporal: bfloat16 [1152, 1152], P('tp'), may hold values from -0.1875 to 0.1875
- fc_in: bfloat16 [1152, 4608], P(None, 'tp'), may hold values from -0.1875 to 0.1875
- fc_out: bfloat16 [4608, 1152], P('tp'), may hold values from -0.09375 to 0.09375
Outputs:
- result: bfloat16 [2, 32, 1024, 1152], P(None, 'seq', 'tp')
All inputs are finite; a program needn't handle non-finite values.
Results may differ from a plain program's by a relative error of at most 0.017.
Values may be sent and summed in bfloat16 or wider, within the bound.
A program may use at most 64 MiB of HBM per device.

v0:
```python
import math

import jax
import jax.numpy as jnp
from jax import lax
from jax.sharding import PartitionSpec as P

D = 1152
H = 16


epsilon = 1e-06


def layer_norm(values):
    average = jnp.mean(values, axis=-1, keepdims=True)
    centred = values - average
    variance = jnp.mean(centred * centred, axis=-1, keepdims=True)
    return centred * lax.rsqrt(variance + epsilon)


def modulated(field, modulation, offset):
    shift_row = modulation[:, offset][:, None, None, :]
    scale_row = modulation[:, offset + 1][:, None, None, :]
    return (layer_norm(field) * (1.0 + scale_row) + shift_row).astype(jnp.bfloat16)


def project_heads(rows_piece, table, gains, head_dim):
    results = []
    for which_part in range(3):
        projected = jnp.einsum(
            "bfpd,de->bfpe", rows_piece, table[which_part], preferred_element_type=jnp.float32
        )
        if which_part < 2:
            shaped = projected.reshape(
                projected.shape[:-1] + (projected.shape[-1] // head_dim, head_dim)
            )
            shaped = (
                shaped
                * lax.rsqrt(jnp.mean(shaped * shaped, axis=-1, keepdims=True) + epsilon)
                * gains[which_part]
            )
            projected = shaped.reshape(projected.shape)
        results.append(projected.astype(jnp.bfloat16))
    return jnp.stack(results)


def attend(query_rows, key_rows, value_rows, head_dim):
    groups, length, feature_width = query_rows.shape
    head_count = feature_width // head_dim
    query_heads = query_rows.reshape(groups, length, head_count, head_dim)
    key_heads = key_rows.reshape(groups, length, head_count, head_dim)
    value_heads = value_rows.reshape(groups, length, head_count, head_dim)
    block_rows = min(length, 512)

    def one_block(first_row):
        query_block = lax.dynamic_slice_in_dim(query_heads, first_row, block_rows, 1)
        scores = jnp.einsum(
            "gqhe,gkhe->ghqk", query_block, key_heads, preferred_element_type=jnp.float32
        ) / math.sqrt(head_dim)
        weights = jnp.exp(scores)
        probabilities = (weights / jnp.sum(weights, axis=-1, keepdims=True)).astype(jnp.bfloat16)
        return jnp.einsum(
            "ghqk,gkhe->gqhe", probabilities, value_heads, preferred_element_type=jnp.float32
        ).astype(jnp.bfloat16)

    starts = jnp.arange(length // block_rows, dtype=jnp.int32) * block_rows
    pieces = lax.map(one_block, starts)
    return pieces.transpose(1, 0, 2, 3, 4).reshape(groups, length, feature_width)


def frame_attention(query_rows, key_rows, value_rows, head_dim):
    batches, frames, patches, feature_width = query_rows.shape
    members = [
        item.transpose(0, 2, 1, 3).reshape(batches * patches, frames, feature_width)
        for item in (query_rows, key_rows, value_rows)
    ]
    mixed_heads = attend(members[0], members[1], members[2], head_dim)
    return mixed_heads.reshape(batches, patches, frames, feature_width).transpose(0, 2, 1, 3)


def body(
    latent,
    modulation,
    qkv_spatial,
    gain_spatial,
    out_spatial,
    qkv_temporal,
    gain_temporal,
    out_temporal,
    fc_in,
    fc_out,
):
    head_dim = D // H
    running = latent.astype(jnp.float32)
    normed = modulated(running, modulation, 0)
    packed = project_heads(
        lax.all_gather(normed, "tp", axis=2, tiled=True), qkv_spatial, gain_spatial, head_dim
    )
    batches, frames, patches, local_width = packed.shape[1:]
    mixed_heads = attend(
        packed[0].reshape(batches * frames, patches, local_width),
        packed[1].reshape(batches * frames, patches, local_width),
        packed[2].reshape(batches * frames, patches, local_width),
        head_dim,
    )
    mixed_heads = mixed_heads.reshape(batches, frames, patches, local_width)
    partial_value = jnp.einsum(
        "bfpe,ed->bfpd", mixed_heads, out_spatial, preferred_element_type=jnp.float32
    )
    spatial_out = lax.psum_scatter(
        partial_value.astype(jnp.bfloat16), "tp", scatter_dimension=2, tiled=True
    )
    running = running + modulation[:, 2][:, None, None, :] * spatial_out.astype(jnp.float32)
    normed = modulated(running, modulation, 3)
    moved_rows = lax.all_to_all(normed, "seq", split_axis=2, concat_axis=1, tiled=True)
    packed = project_heads(
        lax.all_gather(moved_rows, "tp", axis=2, tiled=True), qkv_temporal, gain_temporal, head_dim
    )
    mixed_heads = frame_attention(packed[0], packed[1], packed[2], head_dim)
    partial_value = jnp.einsum(
        "bfpe,ed->bfpd", mixed_heads, out_temporal, preferred_element_type=jnp.float32
    )
    shares = lax.psum_scatter(
        partial_value.astype(jnp.bfloat16), "tp", scatter_dimension=2, tiled=True
    )
    temporal_out = lax.all_to_all(shares, "seq", split_axis=1, concat_axis=2, tiled=True)
    running = running + modulation[:, 5][:, None, None, :] * temporal_out.astype(jnp.float32)
    normed = modulated(running, modulation, 6)
    projected = jnp.einsum(
        "bfpd,de->bfpe",
        lax.all_gather(normed, "tp", axis=2, tiled=True),
        fc_in,
        preferred_element_type=jnp.float32,
    )
    hidden = jax.nn.gelu(projected, approximate=True).astype(jnp.bfloat16)
    partial_value = jnp.einsum("bfpe,ed->bfpd", hidden, fc_out, preferred_element_type=jnp.float32)
    mlp_out = lax.psum_scatter(
        partial_value.astype(jnp.bfloat16), "tp", scatter_dimension=2, tiled=True
    )
    return (running + modulation[:, 8][:, None, None, :] * mlp_out.astype(jnp.float32)).astype(
        jnp.bfloat16
    )


def solution(mesh):
    placed = (
        P(None, "seq", "tp", None),
        P(),
        P(None, None, "tp"),
        P(),
        P("tp", None),
        P(None, None, "tp"),
        P(),
        P("tp", None),
        P(None, "tp"),
        P("tp", None),
    )
    return jax.shard_map(
        body, mesh=mesh, in_specs=placed, out_specs=P(None, "seq", "tp", None), check_vma=False
    )
```

profile of v0, /device:TPU:1, one launch (start us, length us, event | category | flops | bytes accessed | tf_op | source)
XLA Modules:
  0.0 528.2 jit_solution(16318409083778460695)
XLA Ops:
  6.5 0.9 slice_bitcast_fusion.1
  7.5 1.2 convert_reduce_fusion
  8.7 1.4 fusion.58
  10.1 2.2 fusion.61
  12.6 61.0 %all-gather.4.cloned.1.call-done = bf16[2,1,1024,1152]{3,2,0,1:T(8,128)(2,1)} async-done(((bf16[2,1,128,1152]{3,2,0,1:T(8,128)(2,1)}), bf16[2,1,1024,1152]{3,2,0,1:T(8,128)(2,1)}) %all-gather.4.cloned.1.call-update) | async-done | bytes 4718608 | tf_op jit(solution)/shard_map/all_gather | solution.py:98
  73.6 5.1 fusion.93
  78.7 1.4 reduce_sum.111
  80.1 5.5 %fusion.94 = (f32[2,1024,144]{1,2,0:T(8,128)}, f32[2,1024,144]{1,2,0:T(8,128)}) fusion(bf16[3,1152,144]{1,2,0:T(8,128)(2,1)} %param.14, bf16[2,1,1024,1152]{3,2,0,1:T(8,128)(2,1)} %all-gather.4.cloned.1.call-done), kind=kOutput, calls=%fused_computation.130 | convolution fusion | flops 679772160 | bytes 7409664 | tf_op jit(solution)/shard_map/bfpd,de->bfpe/dot_general | solution.py:31
  85.6 1.4 reduce_sum.112
  87.2 1.0 copy-done.4
  88.5 4.9 fusion.55
  93.4 12.8 %while.2 = (s32[]{:T(128)}, bf16[2,2,512,2,72]{2,4,3,1,0:T(8,128)(2,1)S(1)}, s32[2]{0:T(128)S(1)}, bf16[2,1024,2,72]{1,3,2,0:T(8,128)(2,1)S(1)}, bf16[2,1024,2,7...) while((s32[]{:T(128)}, ...), condition=%wide.region_6.7_spmd, body=%wide.region_4.6_spmd.sunk | while | flops 614610944 | bytes 20922552 | solution.py:68
  95.9 1.9 fusion.108
  97.9 1.9 fusion.109
  102.4 1.9 fusion.108
  104.3 1.9 fusion.109
  107.3 3.7 fusion.27
  111.1 58.8 %reduce-scatter.4.cloned.1.call-done = bf16[2,1,128,1152]{3,2,0,1:T(8,128)(2,1)} async-done(((bf16[2,1,1024,1152]{3,2,0,1:T(8,128)(2,1)}), bf16[2,1,128,1152]{3,2,0,1:T(8,128)(2,1)}) %reduce-scatter.4.cloned.1.call-update) | async-done | bytes 589840 | tf_op jit(solution)/shard_map/reduce_scatter | solution.py:111
  169.9 1.4 fusion.73
  171.3 1.4 multiply_reduce_fusion.3
  173.8 28.6 %all_to_all.21 = bf16[2,1,128,1152]{3,0,1,2:T(2,128)(2,1)S(1)} all-to-all(bf16[2,1,128,1152]{3,0,1,2:T(2,128)(2,1)S(1)} %copy.73), channel_id=1, replica_groups=mesh['seq'=32,'tp'=8] {'seq'}, dimensions={2} | all-to-all | bytes 1179648 | tf_op jit(solution)/shard_map/all_to_all | solution.py:116
  204.4 55.5 %all-gather.6.cloned.1.call-done = bf16[2,32,32,1152]{3,1,0,2:T(8,128)(2,1)} async-done(((bf16[2,32,4,1152]{3,1,0,2:T(8,128)(2,1)}), bf16[2,32,32,1152]{3,1,0,2:T(8,128)(2,1)}) %all-gather.6.cloned.1.call-update) | async-done | bytes 4718608 | tf_op jit(solution)/shard_map/all_gather | solution.py:118
  259.8 3.9 fusion.49
  263.7 1.4 reshape_reshape.10
  265.2 3.7 multiply_reduce_fusion
  268.9 3.6 multiply_reduce_fusion.1
  272.6 2.4 multiply_convert_fusion
  275.1 1.2 copy.80
  276.2 1.5 convert_element_type.119
  277.7 1.8 copy.81
  279.5 1.4 reshape_reshape.12
  280.9 2.4 copy.77
  283.3 1.5 convert_element_type.117
  284.8 1.8 copy.78
  286.6 1.4 reshape_reshape.11
  288.1 2.4 fusion.38
  291.2 1.1 copy.86
  292.3 1.5 reshape_reshape_transpose.3
  293.8 3.3 convolution_convert_fusion.1
  297.0 3.8 copy.88
  300.9 58.8 %reduce-scatter.6.cloned.1.call-done = bf16[2,32,4,1152]{3,1,0,2:T(8,128)(2,1)} async-done(((bf16[2,32,32,1152]{3,1,0,2:T(8,128)(2,1)}), bf16[2,32,4,1152]{3,1,0,2:T(8,128)(2,1)}) %reduce-scatter.6.cloned.1.call-update) | async-done | bytes 589840 | tf_op jit(solution)/shard_map/reduce_scatter | solution.py:124
  359.6 1.5 copy.89
  361.2 28.6 %all_to_all.22 = bf16[2,32,4,1152]{3,2,0,1:T(4,128)(2,1)S(1)} all-to-all(bf16[2,32,4,1152]{3,2,0,1:T(4,128)(2,1)S(1)} %copy.89), channel_id=1, replica_groups=mesh['seq'=32,'tp'=8] {'seq'}, dimensions={1} | all-to-all | bytes 1179648 | tf_op jit(solution)/shard_map/all_to_all | solution.py:127
  391.5 1.1 add_convert_fusion.1
  392.7 56.5 %all-gather.8.cloned.1.call-done = bf16[2,1,1024,1152]{3,2,0,1:T(8,128)(2,1)} async-done(((bf16[2,1,128,1152]{3,2,0,1:T(8,128)(2,1)}), bf16[2,1,1024,1152]{3,2,0,1:T(8,128)(2,1)}) %all-gather.8.cloned.1.call-update) | async-done | bytes 4718608 | tf_op jit(solution)/shard_map/all_gather | solution.py:132
  449.1 11.3 %fusion.28 = bf16[2,1,1024,1152]{3,2,0,1:T(8,128)(2,1)} fusion(bf16[2,1,1024,1152]{3,2,0,1:T(8,128)(2,1)} %all-gather.8.cloned.1.call-done, bf16[576,1152]{1,0:T(8,128)(2,1)S(1)} %copy-done, bf16[1152,576]{0,1:T(8,128)(2,1)} %param.20), kind=kOutput, calls=%fused_computation.34 | convolution fusion | flops 5448794112 | bytes 12091392 | tf_op jit(solution)/shard_map/bfpe,ed->bfpd/dot_general | solution.py:137
  460.5 58.8 %reduce-scatter.8.cloned.1.call-done = bf16[2,1,128,1152]{3,2,0,1:T(8,128)(2,1)} async-done(((bf16[2,1,1024,1152]{3,2,0,1:T(8,128)(2,1)}), bf16[2,1,128,1152]{3,2,0,1:T(8,128)(2,1)}) %reduce-scatter.8.cloned.1.call-update) | async-done | bytes 589840 | tf_op jit(solution)/shard_map/reduce_scatter | solution.py:138
  519.3 2.0 fusion.74
  (72 shorter events, 8.6 us)
Async XLA Ops:
  6.5 442.6 %copy-start = (bf16[576,1152]{1,0:T(8,128)(2,1)S(1)}, bf16[576,1152]{1,0:T(8,128)(2,1)}, u32[]{:S(2)}) copy-start(bf16[576,1152]{1,0:T(8,128)(2,1)} %param.21) | copy-start | bytes 3981316
  6.5 5.8 %copy-start.10 = (f32[2,72]{1,0:T(2,128)S(1)}, f32[2,72]{1,0:T(2,128)}, u32[]{:S(2)}) copy-start(f32[2,72]{1,0:T(2,128)} %param.15) | copy-start | bytes 1732
  6.5 67.1 %all-gather.4.cloned.1.call-start = ((), (), s32[]{:S(2)}) async-start(), calls=%async_computation.5 | async-start | bytes 5308416 | tf_op jit(solution)/shard_map/all_gather | solution.py:98
  12.3 157.6 %reduce-scatter.4.cloned.1.call-start = ((), (), s32[]{:S(2)}) async-start(), calls=%async_computation.6 | async-start | bytes 5308416 | tf_op jit(solution)/shard_map/reduce_scatter | solution.py:111
  87.0 1.3 copy-start.4
  88.5 5.0 copy-start.6
  95.9 2.0 copy-start.12
  102.4 2.0 copy-start.12
  106.3 1.1 copy-start.8
  111.0 58.9 %copy-start.1 = (bf16[2,1,128,1152]{3,2,1,0:T(8,128)(2,1)S(1)}, bf16[2,1,128,1152]{3,2,1,0:T(8,128)(2,1)}, u32[]{:S(2)}) copy-start(bf16[2,1,128,1152]{3,2,1,0:T(8,128)(2,1)} %param.12) | copy-start | bytes 1769476
  111.1 148.8 %all-gather.6.cloned.1.call-start = ((), (), s32[]{:S(2)}) async-start(), calls=%async_computation.7 | async-start | bytes 5308416 | tf_op jit(solution)/shard_map/all_gather | solution.py:118
  169.9 2.9 copy-start.2
  173.2 30.4 %copy-start.11 = (f32[2,72]{1,0:T(2,128)S(1)}, f32[2,72]{1,0:T(2,128)}, u32[]{:S(2)}) copy-start(f32[2,72]{1,0:T(2,128)} %param.18) | copy-start | bytes 1732
  173.2 30.4 %copy-start.7 = (bf16[3,1152,144]{1,2,0:T(8,128)(2,1)S(1)}, bf16[3,1152,144]{1,2,0:T(8,128)(2,1)}, u32[]{:S(2)}) copy-start(bf16[3,1152,144]{1,2,0:T(8,128)(2,1)} %param.17) | copy-start | bytes 2985988
  203.3 156.3 %reduce-scatter.6.cloned.1.call-start = ((), (), s32[]{:S(2)}) async-start(), calls=%async_computation.8 | async-start | bytes 5308416 | tf_op jit(solution)/shard_map/reduce_scatter | solution.py:124
  288.1 2.4 copy-start.5
  291.2 2.6 copy-start.9
  300.8 148.3 %all-gather.8.cloned.1.call-start = ((), (), s32[]{:S(2)}) async-start(), calls=%async_computation.9 | async-start | bytes 5308416 | tf_op jit(solution)/shard_map/all_gather | solution.py:132
  389.7 1.1 copy-start.3
  392.6 126.7 %reduce-scatter.8.cloned.1.call-start = ((), (), s32[]{:S(2)}) async-start(), calls=%async_computation.10 | async-start | bytes 5308416 | tf_op jit(solution)/shard_map/reduce_scatter | solution.py:138
Sparse Core Ops, SparseCore 0:
  12.4 61.1 all-gather.3
  111.2 58.6 reduce-scatter.3
  203.4 56.3 all-gather.5
  300.9 58.6 reduce-scatter.5
  392.8 56.3 all-gather.7
  460.6 58.6 reduce-scatter.7
where the time goes:
time: 530 us; the launch traced here: 528 us
  waiting for transfers between devices  349 us (66%)
  blocking collectives  57.2 us (11%)
  matrix products  55.9 us (11%)
  local copies, waits for them, and re-layouts  28.9 us (5%)
  other arithmetic  18.6 us (4%)
  between operations  13.8 us (3%)
    reduce_scatter x3, waiting for transfers between devices, body(): lax.psum_scatter(partial_value.astype(jnp.bfloat16), 'tp', scatter_dimens...  176 us
    all_gather x2, waiting for transfers between devices, body(): lax.all_gather(normed, 'tp', axis=2, tiled=True)  118 us
    all_gather x1, waiting for transfers between devices, body(): lax.all_gather(moved_rows, 'tp', axis=2, tiled=True)  55.5 us
    all_to_all x1, blocking collectives, body(): lax.all_to_all(normed, 'seq', split_axis=2, concat_axis=1, tiled=True)  28.6 us
    all_to_all x1, blocking collectives, body(): lax.all_to_all(shares, 'seq', split_axis=1, concat_axis=2, tiled=True)  28.6 us
    dot_general x6, matrix products, project_heads(): jnp.einsum('bfpd,de->bfpe', rows_piece, table[which_part], preferred_elem...  26.8 us
    dot_general x1, matrix products, body(): jnp.einsum('bfpe,ed->bfpd', hidden, fc_out, preferred_element_type=jnp.fl...  11.3 us
  transfers between devices with their start and end apart: 6, of which 6 were waited for; matrix products, arithmetic and copies ran while one was open for 0% of the time, Pallas kernels for 0%

commit v1 on v0

v1 whole, which is shorter than its diff:
```python
import math

import jax
import jax.numpy as jnp
from jax import lax
from jax.experimental import pallas as pl
from jax.experimental.pallas import tpu as pltpu
from jax.sharding import PartitionSpec as P

D = 1152
H = 16
HD = 72
HW = 144
N_TP = 8
N_SEQ = 32
ROUNDS = 4
MESH = pl.DeviceIdType.MESH
EPS = 1e-06
SCALE = 1.0 / math.sqrt(HD)
F32 = jnp.float32
BF16 = jnp.bfloat16

O_S, QKV_T, O_T, FC1, FC2, END = 0, 9, 36, 45, 81, 117


def layer_norm(values):
    average = jnp.mean(values, axis=-1, keepdims=True)
    centred = values - average
    variance = jnp.mean(centred * centred, axis=-1, keepdims=True)
    return centred * lax.rsqrt(variance + EPS)


def dot(left, right, left_dim=1, right_dim=0):
    return lax.dot_general(
        left, right, (((left_dim,), (right_dim,)), ((), ())), preferred_element_type=F32
    )


def head_norm_rows(values, gain):
    halves = []
    for head in range(2):
        part = values[head * HD : (head + 1) * HD]
        halves.append(part * lax.rsqrt(jnp.mean(part * part, axis=0, keepdims=True) + EPS))
    return jnp.concatenate(halves, axis=0) * gain


def head_norm_lanes(values, gain):
    first = lax.broadcasted_iota(jnp.int32, values.shape, 1) < HD
    square = values * values
    low = jnp.sum(jnp.where(first, square, 0.0), axis=-1, keepdims=True)
    high = jnp.sum(jnp.where(first, 0.0, square), axis=-1, keepdims=True)
    factor = jnp.where(
        first, lax.rsqrt(low * (1.0 / HD) + EPS), lax.rsqrt(high * (1.0 / HD) + EPS)
    )
    return values * factor * gain


def remote(src, dst, send_sem, recv_sem, seq, tp):
    return pltpu.make_async_remote_copy(
        src_ref=src,
        dst_ref=dst,
        send_sem=send_sem,
        recv_sem=recv_sem,
        device_id={"seq": seq, "tp": tp},
        device_id_type=MESH,
    )


def greet(peers):
    barrier = pltpu.get_barrier_semaphore()
    for seq, tp in peers:
        pl.semaphore_signal(
            barrier, inc=1, device_id={"seq": seq, "tp": tp}, device_id_type=MESH
        )
    pl.semaphore_wait(barrier, len(peers))


def spatial_kernel(
    lat,
    mod,
    wqkv,
    gcol,
    grow,
    wsh,
    mid,
    nrm,
    g,
    xs,
    ks,
    qs,
    vs,
    ot,
    heads,
    wos,
    ag_send,
    ag_recv,
    s1_send,
    s1_recv,
    own_sem,
    w_send,
    w_recv,
    d_send,
    d_recv,
    h_send,
    h_recv,
    os_sem,
):
    seq, me = lax.axis_index("seq"), lax.axis_index("tp")
    x, zh, y = seq // 8, lax.rem(seq // 4, 2), lax.rem(seq, 4)
    zl, c = me // 2, lax.rem(me, 2)
    sib = zl * 2 + (1 - c)

    def xy(dx, dy):
        return (lax.rem(x + dx + 4, 4) * 2 + zh) * 4 + lax.rem(y + dy + 4, 4)

    def zdev(dz, core):
        z = lax.rem(zh * 4 + zl + dz + 8, 8)
        return (x * 2 + z // 4) * 4 + y, lax.rem(z, 4) * 2 + core

    ring = (xy(1, 0), xy(-1, 0), xy(0, 1), xy(0, -1))
    z_targets = [zdev(dz, core) for dz in (1, -1, 2) for core in range(2)]
    peers = [(seq, lax.rem(me + i, N_TP)) for i in range(1, N_TP)]
    peers += [(to, me) for to in ring]
    peers += [zdev(dz, core) for dz in (1, -1, 2, -2) for core in range(2)]
    greet(peers)

    def s1_copies(k):
        copies = []
        for i, (to_seq, to_tp) in enumerate(z_targets):
            unit = (x * 4 + y) * 2 + i % 2
            copies.append(
                remote(
                    wsh.at[k, unit],
                    g.at[me, k, x, y, i % 2],
                    s1_send.at[k, i],
                    s1_recv.at[k, me],
                    to_seq,
                    to_tp,
                )
            )
        copies.append(
            remote(
                wsh.at[k, (x * 4 + y) * 2 + (1 - c)],
                g.at[me, k, x, y, 1 - c],
                s1_send.at[k, 6],
                s1_recv.at[k, me],
                seq,
                sib,
            )
        )
        return copies

    def own_copy(k):
        return pltpu.make_async_copy(
            wsh.at[k, (x * 4 + y) * 2 + c], g.at[me, k, x, y, c], own_sem.at[k]
        )

    def s1_start(k):
        own_copy(k).start()
        for copy in s1_copies(k):
            copy.start()

    def s1_wait(k):
        own_copy(k).wait()
        for i in range(1, N_TP):
            source = lax.rem(me + i, N_TP)
            spot = g.at[source, k, x, y, c]
            remote(spot, spot, s1_send.at[k, 0], s1_recv.at[k, source], seq, sib).wait_recv()

    left, right = pl.ds(0, 4), pl.ds(4, 4)
    x_back, x_next = lax.rem(x + 3, 4), lax.rem(x + 1, 4)
    y_back, y_next = lax.rem(y + 3, 4), lax.rem(y + 1, 4)

    def ring_copies(stage, k):
        if stage == 0:
            spots = [g.at[left, k, x, y, c]] * 2 + [g.at[right, k, x, y, c]] * 2
        elif stage == 1:
            spots = [
                g.at[pl.ds(0, 2), k, x_back, y, c],
                g.at[pl.ds(2, 2), k, x_next, y, c],
                g.at[pl.ds(4, 2), k, x, y_back, c],
                g.at[pl.ds(6, 2), k, x, y_next, c],
            ]
        elif stage == 2:
            spots = [g.at[right, k, x, :, c]] * 2 + [g.at[left, k, :, y, c]] * 2
        else:
            spots = [
                g.at[pl.ds(4, 2), k, x_back, :, c],
                g.at[pl.ds(6, 2), k, x_next, :, c],
                g.at[pl.ds(0, 2), k, :, y_back, c],
                g.at[pl.ds(2, 2), k, :, y_next, c],
            ]
        return [
            remote(spot, spot, w_send.at[stage, k, i], w_recv.at[stage, k, i], ring[i], me)
            for i, spot in enumerate(spots)
        ]

    def ring_start(stage, k):
        for copy in ring_copies(stage, k):
            copy.start()

    def ring_wait(stage, k):
        for copy in ring_copies(stage, k):
            copy.wait_recv()

    def core_copy(k):
        spot = g.at[:, k, :, :, c]
        return remote(spot, spot, d_send.at[k], d_recv.at[k], seq, sib)

    def pump(step, k):
        if step == 0:
            s1_start(k)
        elif step == 1:
            s1_wait(k)
            ring_start(0, k)
        elif step <= 4:
            ring_wait(step - 2, k)
            ring_start(step - 1, k)
        elif step == 5:
            ring_wait(3, k)
            core_copy(k).start()
        else:
            core_copy(k).wait_recv()

    def ag_copy(slot, b, way):
        to = (jnp.minimum(zl + 1, 3) * 2 + c, jnp.maximum(zl - 1, 0) * 2 + c, sib)[way]
        spot = xs.at[slot, b]
        return remote(spot, spot, ag_send.at[slot, b, way], ag_recv.at[slot, b], seq, to)

    def ag_step(distance, b, what):
        for way in range(2):
            origin = zl - distance if way == 0 else zl + distance
            there = (zl >= distance) if way == 0 else (zl + distance <= 3)
            more = (zl < 3) if way == 0 else (zl > 0)
            if distance == 0:
                there = more
            slot = origin * 2 + c

            @pl.when(there)
            def _():
                if what == 0 and distance > 0:
                    ag_copy(slot, b, 2).wait_recv()
                if distance == 0:
                    copy = ag_copy(slot, b, way)
                    copy.start() if what == 0 else copy.wait_send()
                else:

                    @pl.when(more)
                    def _():
                        copy = ag_copy(slot, b, way)
                        copy.start() if what == 0 else copy.wait_send()

                    copy = ag_copy(slot, b, 2)
                    copy.start() if what == 0 else copy.wait_send()

        if distance == 0:
            copy = ag_copy(me, b, 2)
            copy.start() if what == 0 else copy.wait_send()

    def project(z):
        rows = xs[pl.ds(z * 2, 2)].reshape(512, D)
        queries = head_norm_rows(dot(wqkv[0], rows, 1, 1), gcol[...]).astype(BF16)
        values = dot(wqkv[2], rows, 1, 1).astype(BF16)
        keys = head_norm_lanes(dot(rows, wqkv[1], 1, 1), grow[...]).astype(BF16)
        for core in range(2):
            for b in range(2):
                at = (core * 2 + b) * 128
                qs[b, z * 2 + core] = queries[:, at : at + 128]
                spot = pl.ds(pl.multiple_of((z * 2 + core) * 128, 128), 128)
                vs[b, :, spot] = values[:, at : at + 128]
                ks[b, z * 2 + core] = keys[at : at + 128]

    def head_copy(b, to):
        return remote(
            ot.at[b, to], heads.at[b, me], h_send.at[b, to], h_recv.at[b, me], seq, to
        )

    def attend(b):
        keys = ks[b].reshape(N_TP * 128, HW)
        values = vs[b]

        def block(i, _):
            to = lax.rem(me + 1 + i, N_TP)
            query = qs[b, to]
            zero = jnp.zeros((HD, 128), BF16)
            pair = jnp.concatenate(
                [
                    jnp.concatenate([query[:HD].astype(F32), zero.astype(F32)], axis=0),
                    jnp.concatenate([zero.astype(F32), query[HD:].astype(F32)], axis=0),
                ],
                axis=1,
            ).astype(BF16)
            weights = jnp.exp(dot(keys, pair) * SCALE)
            total = jnp.sum(weights, axis=0, keepdims=True)
            mixed = dot(values, weights.astype(BF16)) / total
            result = jnp.concatenate([mixed[:HD, :128], mixed[HD:, 128:]], axis=0).astype(BF16)

            @pl.when(to != me)
            def _():
                ot[b, to] = result
                head_copy(b, to).start()

            @pl.when(to == me)
            def _():
                heads[b, me] = result

            return 0

        lax.fori_loop(0, N_TP, block, 0)

    def finish(b):
        for i in range(1, N_TP):
            source = lax.rem(me + i, N_TP)
            spot = heads.at[b, source]
            remote(spot, spot, h_send.at[b, source], h_recv.at[b, source], seq, source).wait_recv()
        mixed = heads[b].reshape(D, 128).T
        out = dot(mixed, wos[...].reshape(D, D)).astype(BF16).astype(F32)
        rows = pl.ds(b * 128, 128)
        late = lat[rows].astype(F32) + mod[b, 2:3] * out
        mid[rows] = late
        normed = layer_norm(late) * (1.0 + mod[b, 4:5]) + mod[b, 3:4]
        nrm[pl.ds(b * 16, 16)] = normed.reshape(16, 8, D).astype(BF16)

    pump(0, 0)
    for b in range(2):
        rows = lat[pl.ds(b * 128, 128)].astype(F32)
        xs[me, b] = (layer_norm(rows) * (1.0 + mod[b, 1:2]) + mod[b, 0:1]).astype(BF16)
        ag_step(0, b, 0)
    pump(0, 1)
    for b in range(2):
        ag_copy(sib, b, 2).wait_recv()
    project(zl)
    pump(1, 0)
    ag_step(1, 0, 0)
    pump(2, 0)
    ag_step(1, 1, 0)
    pump(0, 2)
    pump(1, 1)
    pump(3, 0)
    ag_step(2, 0, 0)
    pump(0, 3)
    pump(2, 1)
    ag_step(2, 1, 0)
    pump(3, 1)
    pump(1, 2)
    pump(4, 0)
    ag_step(3, 0, 0)
    pump(2, 2)
    ag_step(3, 1, 0)
    for distance in range(1, 4):
        for b in range(2):
            other = lax.rem(zl + distance, 4) * 2 + (1 - c)
            ag_copy(other, b, 2).wait_recv()
    for i in range(1, 4):
        project(lax.rem(zl + i, 4))
    pump(1, 3)
    attend(0)
    pump(5, 0)
    pump(4, 1)
    pump(3, 2)
    pump(2, 3)
    attend(1)
    pump(6, 0)
    os_copies = [
        pltpu.make_async_copy(g.at[:, 0, 0, i], wos.at[:, pl.ds(2 * i, 2)], os_sem.at[i])
        for i in range(4)
    ] + [pltpu.make_async_copy(g.at[:, 0, 1, 0, 0], wos.at[:, 8], os_sem.at[4])]
    for copy in os_copies:
        copy.start()
    for copy in os_copies:
        copy.wait()
    finish(0)
    finish(1)
    pump(5, 1)
    pump(4, 2)
    pump(3, 3)
    pump(6, 1)
    pump(5, 2)
    pump(4, 3)
    pump(6, 2)
    pump(5, 3)
    pump(6, 3)

    for b in range(2):
        for distance in range(4):
            ag_step(distance, b, 1)
        for i in range(1, N_TP):
            head_copy(b, lax.rem(me + i, N_TP)).wait_send()
    for k in range(ROUNDS):
        for copy in s1_copies(k):
            copy.wait_send()
        for stage in range(4):
            for copy in ring_copies(stage, k):
                copy.wait_send()
        core_copy(k).wait_send()


def temporal_kernel(
    nrm,
    mid,
    mod,
    gcol,
    grow,
    g,
    result,
    rows_in,
    rows_out,
    rows_back,
    ot,
    wqkv,
    wo,
    w1,
    w2,
    late,
    f_send,
    f_recv,
    b_send,
    b_recv,
    w_sem,
):
    seq, me = lax.axis_index("seq"), lax.axis_index("tp")
    loads = [
        pltpu.make_async_copy(g.at[:, pl.ds(QKV_T, 27)], wqkv, w_sem.at[0]),
        pltpu.make_async_copy(g.at[:, pl.ds(O_T, 9)], wo, w_sem.at[1]),
        pltpu.make_async_copy(g.at[:, pl.ds(FC1, 36)], w1, w_sem.at[2]),
        pltpu.make_async_copy(g.at[:, pl.ds(FC2, 36)], w2, w_sem.at[3]),
    ]
    for load in loads:
        load.start()
    greet([(lax.rem(seq + i, N_SEQ), me) for i in range(1, N_SEQ)])

    def exchange(source, target, send, recv):
        def start(i, _):
            to = lax.rem(seq + i, N_SEQ)
            remote(source.at[to], target.at[seq], send.at[to], recv.at[seq], to, me).start()
            return 0

        lax.fori_loop(1, N_SEQ, start, 0)
        target[seq] = source[seq]

        def finish(i, _):
            sender = lax.rem(seq + i, N_SEQ)
            spot = target.at[sender]
            remote(spot, spot, send.at[sender], recv.at[sender], sender, me).wait_recv()
            return 0

        lax.fori_loop(1, N_SEQ, finish, 0)

    def drain(source, send, recv):
        def finish(i, _):
            to = lax.rem(seq + i, N_SEQ)
            spot = source.at[to]
            remote(spot, spot, send.at[to], recv.at[to], to, me).wait_send()
            return 0

        lax.fori_loop(1, N_SEQ, finish, 0)

    exchange(nrm, rows_in, f_send, f_recv)
    rows = rows_in[...].astype(F32).reshape(256, D).astype(BF16)
    same = (
        lax.rem(lax.broadcasted_iota(jnp.int32, (256, 256), 0), 8)
        == lax.rem(lax.broadcasted_iota(jnp.int32, (256, 256), 1), 8)
    )
    loads[0].wait()

    def pair_of_heads(t, _):
        weights = wqkv[t].reshape(3 * HW, D)
        queries = head_norm_rows(dot(weights[:HW], rows, 1, 1), gcol[...])
        keys = head_norm_lanes(dot(rows, weights[HW : 2 * HW], 1, 1), grow[...]).astype(BF16)
        values = dot(weights[2 * HW :], rows, 1, 1).astype(BF16)
        parts = []
        zero = jnp.zeros((HD, 256), F32)
        for head in range(2):
            kept = queries[head * HD : (head + 1) * HD]
            kept = jnp.concatenate([kept, zero] if head == 0 else [zero, kept], axis=0)
            scores = dot(keys, kept.astype(BF16)) * SCALE
            probs = jnp.where(same, jnp.exp(scores), 0.0)
            total = jnp.sum(probs, axis=0, keepdims=True)
            mixed = dot(values, probs.astype(BF16)) / total
            parts.append(mixed[head * HD : (head + 1) * HD])
        ot[t] = jnp.concatenate(parts, axis=0).astype(BF16)
        return 0

    lax.fori_loop(0, N_TP, pair_of_heads, 0)
    loads[1].wait()
    mixed = ot[...].reshape(D, 256).T
    out = dot(mixed, wo[...].reshape(D, D))
    rows_out[...] = out.reshape(N_SEQ, 8, D).astype(BF16)
    exchange(rows_out, rows_back, b_send, b_recv)
    back = rows_back[...].astype(F32).reshape(256, D)
    normed = []
    for b in range(2):
        part = mid[pl.ds(b * 128, 128)] + mod[b, 5:6] * back[b * 128 : (b + 1) * 128]
        late[pl.ds(b * 128, 128)] = part
        normed.append(layer_norm(part) * (1.0 + mod[b, 7:8]) + mod[b, 6:7])
    normed = jnp.concatenate(normed, axis=0).astype(BF16)
    loads[2].wait()
    loads[3].wait()

    def hidden_chunk(t, total):
        u = dot(normed, w1[t].reshape(576, D), 1, 1)
        h = 0.5 * u * (1.0 + jnp.tanh(math.sqrt(2.0 / math.pi) * (u + 0.044715 * (u * u * u))))
        return total + dot(h.astype(BF16), w2[t].reshape(576, D))

    total = lax.fori_loop(0, N_TP, hidden_chunk, jnp.zeros((256, D), F32))
    total = total.astype(BF16).astype(F32)
    for b in range(2):
        at = pl.ds(b * 128, 128)
        result[at] = (late[at] + mod[b, 8:9] * total[b * 128 : (b + 1) * 128]).astype(BF16)
    drain(nrm, f_send, f_recv)
    drain(rows_out, b_send, b_recv)


def body(
    latent,
    modulation,
    qkv_spatial,
    gain_spatial,
    out_spatial,
    qkv_temporal,
    gain_temporal,
    out_temporal,
    fc_in,
    fc_out,
):
    def gains(table):
        column = jnp.tile(table[0], 2).reshape(HW, 1)
        row = jnp.tile(table[1], 2).reshape(1, HW)
        return column, row

    sizes = (144, 432, 144, 576, 576)
    pieces = [
        out_spatial,
        qkv_temporal.transpose(0, 2, 1).reshape(432, D),
        out_temporal,
        fc_in.T,
        fc_out,
        jnp.zeros((2048 - sum(sizes), D), BF16),
    ]
    wsh = jnp.concatenate(pieces, axis=0).reshape(ROUNDS, 32, 16, D)
    vmem = pl.BlockSpec(memory_space=pltpu.VMEM)
    hbm = pl.BlockSpec(memory_space=pl.ANY)
    dma = pltpu.SemaphoreType.DMA
    gcol, grow = gains(gain_spatial)
    mid, nrm, g = pl.pallas_call(
        spatial_kernel,
        name="spatial",
        out_shape=(
            jax.ShapeDtypeStruct((256, D), F32),
            jax.ShapeDtypeStruct((N_SEQ, 8, D), BF16),
            jax.ShapeDtypeStruct((N_TP, ROUNDS, 4, 4, 2, 16, D), BF16),
        ),
        in_specs=[vmem] * 5 + [hbm],
        out_specs=(vmem, vmem, hbm),
        scratch_shapes=[
            pltpu.VMEM((N_TP, 2, 128, D), BF16),
            pltpu.VMEM((2, N_TP, 128, HW), BF16),
            pltpu.VMEM((2, N_TP, HW, 128), BF16),
            pltpu.VMEM((2, HW, 1024), BF16),
            pltpu.VMEM((2, N_TP, HW, 128), BF16),
            pltpu.VMEM((2, N_TP, HW, 128), BF16),
            pltpu.VMEM((N_TP, 9, 16, D), BF16),
            dma((N_TP, 2, 3)),
            dma((N_TP, 2)),
            dma((ROUNDS, 7)),
            dma((ROUNDS, N_TP)),
            dma((ROUNDS,)),
            dma((4, ROUNDS, 4)),
            dma((4, ROUNDS, 4)),
            dma((ROUNDS,)),
            dma((ROUNDS,)),
            dma((2, N_TP)),
            dma((2, N_TP)),
            dma((5,)),
        ],
        compiler_params=pltpu.CompilerParams(
            collective_id=0, has_side_effects=True, vmem_limit_bytes=48 << 20
        ),
    )(
        latent.reshape(256, D),
        modulation,
        qkv_spatial.transpose(0, 2, 1),
        gcol,
        grow,
        wsh,
    )
    gcol, grow = gains(gain_temporal)
    result = pl.pallas_call(
        temporal_kernel,
        name="temporal",
        out_shape=jax.ShapeDtypeStruct((256, D), BF16),
        in_specs=[vmem] * 5 + [hbm],
        out_specs=vmem,
        scratch_shapes=[
            pltpu.VMEM((N_SEQ, 8, D), BF16),
            pltpu.VMEM((N_SEQ, 8, D), BF16),
            pltpu.VMEM((N_SEQ, 8, D), BF16),
            pltpu.VMEM((N_TP, HW, 256), BF16),
            pltpu.VMEM((N_TP, 27, 16, D), BF16),
            pltpu.VMEM((N_TP, 9, 16, D), BF16),
            pltpu.VMEM((N_TP, 36, 16, D), BF16),
            pltpu.VMEM((N_TP, 36, 16, D), BF16),
            pltpu.VMEM((256, D), F32),
            dma((N_SEQ,)),
            dma((N_SEQ,)),
            dma((N_SEQ,)),
            dma((N_SEQ,)),
            dma((4,)),
        ],
        compiler_params=pltpu.CompilerParams(
            collective_id=1, has_side_effects=True, vmem_limit_bytes=60 << 20
        ),
    )(nrm, mid, modulation, gcol, grow, g.reshape(N_TP, 128, 16, D))
    return result.reshape(latent.shape)


def solution(mesh):
    placed = (
        P(None, "seq", "tp", None),
        P(),
        P(None, None, "tp"),
        P(),
        P("tp", None),
        P(None, None, "tp"),
        P(),
        P("tp", None),
        P(None, "tp"),
        P("tp", None),
    )
    return jax.shard_map(
        body, mesh=mesh, in_specs=placed, out_specs=P(None, "seq", "tp", None), check_vma=False
    )
```

time: 530 us -> 222 us (0.42)
  waiting for transfers between devices: 349 us -> 0 us
  Pallas kernels: 0 us -> 206 us
  blocking collectives: 57.2 us -> 0 us
  matrix products: 55.9 us -> 0 us
  other arithmetic: 18.6 us -> 0 us
  local copies, waits for them, and re-layouts: 28.9 us -> 14.5 us
  between operations: 13.8 us -> 0.12 us
    pallas_call x0 -> x2, Pallas kernels: none -> 206 us  [the longest x1 147 us: body(): pl.pallas_call(spatial_kernel, name='spatial', out_shape=(jax.ShapeDtypeS...]
    reduce_scatter x3 -> x0, waiting for transfers between devices: 176 us -> none  [body(): lax.psum_scatter(partial_value.astype(jnp.bfloat16), 'tp', scatter_dimens...]
    all_gather x3 -> x0, waiting for transfers between devices: 173 us -> none  [the longest x2 118 us: body(): lax.all_gather(normed, 'tp', axis=2, tiled=True)]
    all_to_all x2 -> x0, blocking collectives: 57.2 us -> none  [the longest x1 28.6 us: body(): lax.all_to_all(normed, 'seq', split_axis=2, concat_axis=1, tiled=True)]
    dot_general x15 -> x0, matrix products: 55.9 us -> none  [the longest x6 26.8 us: project_heads(): jnp.einsum('bfpd,de->bfpe', rows_piece, table[which_part], preferred_elem...]
    convert_element_type x8 -> x0, local copies, waits for them, and re-layouts: 12.9 us -> none  [the longest x4 6.51 us: project_heads(): results.append(projected.astype(jnp.bfloat16))]
    unnamed x24 -> x23, local copies, waits for them, and re-layouts: 1.14 us -> 12.1 us
    reduce_sum x8 -> x0, other arithmetic: 8.82 us -> none  [the longest x3 3.05 us: layer_norm(): variance = jnp.mean(centred * centred, axis=-1, keepdims=True)]
  transfers between devices with their start and end apart: 6 -> 0, of which waited for: 6 -> 0; matrix products, arithmetic and copies ran while one was open for 0% -> 0% of each run, Pallas kernels for 0% -> 0%
where the time goes in v1:
time: 222 us; the launch traced here: 221 us
  Pallas kernels  206 us (93%)
  local copies, waits for them, and re-layouts  14.5 us (7%)
    pallas_call x1, Pallas kernels, body(): pl.pallas_call(spatial_kernel, name='spatial', out_shape=(jax.ShapeDtypeS...  147 us
    pallas_call x1, Pallas kernels, body(): pl.pallas_call(temporal_kernel, name='temporal', out_shape=jax.ShapeDtype...  59.6 us
    unnamed x23, local copies, waits for them, and re-layouts  12.1 us

profile of v1, /device:TPU:1, one launch (start us, length us, event | category | flops | bytes accessed | tf_op | source)
XLA Modules:
  0.0 221.1 jit_solution(991990410901128042)
XLA Ops:
  0.0 0.0 copy-start.6
  0.0 0.0 copy-start.3
  0.0 0.0 copy-start.2
  0.0 1.1 copy.14.mod
  1.1 0.0 copy-start
  1.1 0.8 slice_bitcast_fusion.2
  1.8 0.1 reshape_tile.16.gcol
  2.0 0.1 reshape_tile.13.grow
  2.1 1.0 constant_dynamic-update-slice_fusion.3
  3.1 1.3 constant_dynamic-update-slice_fusion.2
  4.4 1.0 constant_dynamic-update-slice_fusion.1
  5.4 1.5 bitcast_dynamic-update-slice_fusion
  7.0 0.0 copy-done.6
  7.0 0.0 copy-start.7
  7.0 0.2 constant_dynamic-update-slice_fusion
  7.2 0.0 copy-start.5
  7.2 2.2 copy-done.5
  9.4 0.0 copy-done.3
  9.4 0.0 copy-done.2
  9.4 146.9 %spatial.1 = (f32[256,1152]{1,0:T(8,128)S(1)}, bf16[32,8,1152]{2,1,0:T(8,128)(2,1)S(1)}, bf16[8,4,4,4,2,16,1152]{6,5,4,3,2,1,0:T(8,128)(2,1)}) custom-call(bf16[256,1152]{1,0:T(8,128)(2,1)S(1)} %bitcast.21, f32[2,9,1152]{2,1,0:T(8,128)S(1)} %copy.14.mod, bf16[3,144,1152]{2,1,0:T(8,128)(2,1)S(1)} %bitcast.20, f32[144,1]{1,0:T(8,128)S(1)} %reshape_tile.16.gcol, ...), custom_call_target="tpu_custom_call" | custom-call | tf_op jit(solution)/shard_map/spatial/pallas_call | solution.py:545
  156.3 0.0 copy-done
  156.3 0.0 copy-start.1
  156.3 1.0 copy-done.1
  157.4 0.0 copy-start.4
  157.4 0.8 copy-done.4
  158.2 0.0 copy-done.7
  158.2 0.8 reshape_tile.17.gcol
  159.0 0.6 reshape_tile.15.grow
  159.6 59.6 %temporal.1 = bf16[256,1152]{1,0:T(8,128)(2,1)} custom-call(bf16[32,8,1152]{2,1,0:T(8,128)(2,1)} %copy-done.4, f32[256,1152]{1,0:T(8,128)} %copy-done.1, f32[2,9,1152]{2,1,0:T(8,128)} %copy-done, f32[144,1]{1,0:T(8,128)} %reshape_tile.17.gcol, f32[1,144]{1,0:T(1,128)} %reshape_tile.15.grow, bf16[8,128,16,1152]{3,2,1,0:T(8,128)(2,1)} %bitcast.22), custom_call_target="tpu_custom_call" | custom-call | tf_op jit(solution)/shard_map/temporal/pallas_call | solution.py:588
  219.1 1.9 copy.25
  (6 shorter events, 0.1 us)
Async XLA Ops:
  0.0 7.0 %copy-start.6 = (bf16[576,1152]{1,0:T(8,128)(2,1)S(1)}, bf16[576,1152]{1,0:T(8,128)(2,1)}, u32[]{:S(2)}) copy-start(bf16[576,1152]{1,0:T(8,128)(2,1)} %param.19) | copy-start | bytes 3981316
  0.0 9.4 %copy-start.3 = (bf16[2,1,128,1152]{3,2,1,0:T(8,128)(2,1)S(1)}, bf16[2,1,128,1152]{3,2,1,0:T(8,128)(2,1)}, u32[]{:S(2)}) copy-start(bf16[2,1,128,1152]{3,2,1,0:T(8,128)(2,1)} %param.10) | copy-start | bytes 1769476
  0.0 9.4 %copy-start.2 = (bf16[3,1152,144]{1,2,0:T(8,128)(2,1)S(1)}, bf16[3,1152,144]{1,2,0:T(8,128)(2,1)}, u32[]{:S(2)}) copy-start(bf16[3,1152,144]{1,2,0:T(8,128)(2,1)} %param.12) | copy-start | bytes 2985988
  1.1 155.3 %copy-start = (f32[2,9,1152]{2,1,0:T(8,128)}, f32[2,9,1152]{2,1,0:T(8,128)S(1)}, u32[]{:S(2)}) copy-start(f32[2,9,1152]{2,1,0:T(8,128)S(1)} %copy.14.mod) | copy-start | bytes 248836
  7.0 151.2 %copy-start.7 = (f32[2,72]{1,0:T(2,128)S(1)}, f32[2,72]{1,0:T(2,128)}, u32[]{:S(2)}) copy-start(f32[2,72]{1,0:T(2,128)} %param.16) | copy-start | bytes 1732
  7.2 2.2 copy-start.5
  156.3 1.0 copy-start.1
  157.4 0.8 copy-start.4

commit v2 on v0

v2 whole, which is shorter than its diff:
```python
import math

import jax
import jax.numpy as jnp
from jax import lax
from jax.experimental import pallas as pl
from jax.experimental.pallas import tpu as pltpu
from jax.sharding import PartitionSpec as P

D = 1152
H = 16
HD = 72
HW = 144
N_TP = 8
N_SEQ = 32
MESH = pl.DeviceIdType.MESH
EPS = 1e-06
SCALE = 1.0 / math.sqrt(HD)
F32 = jnp.float32
BF16 = jnp.bfloat16

ATT = 2
ROUNDS = 5


def layer_norm(values):
    average = jnp.mean(values, axis=-1, keepdims=True)
    centred = values - average
    variance = jnp.mean(centred * centred, axis=-1, keepdims=True)
    return centred * lax.rsqrt(variance + EPS)


def dot(left, right, left_dim=1, right_dim=0):
    return lax.dot_general(
        left, right, (((left_dim,), (right_dim,)), ((), ())), preferred_element_type=F32
    )


def head_norm_rows(values, gain):
    halves = []
    for head in range(2):
        part = values[head * HD : (head + 1) * HD]
        halves.append(part * lax.rsqrt(jnp.mean(part * part, axis=0, keepdims=True) + EPS))
    return jnp.concatenate(halves, axis=0) * gain


def head_norm_lanes(values, gain):
    first = lax.broadcasted_iota(jnp.int32, values.shape, 1) < HD
    square = values * values
    low = jnp.sum(jnp.where(first, square, 0.0), axis=-1, keepdims=True)
    high = jnp.sum(jnp.where(first, 0.0, square), axis=-1, keepdims=True)
    factor = jnp.where(
        first, lax.rsqrt(low * (1.0 / HD) + EPS), lax.rsqrt(high * (1.0 / HD) + EPS)
    )
    return values * factor * gain


def remote(src, dst, send_sem, recv_sem, seq, tp):
    return pltpu.make_async_remote_copy(
        src_ref=src,
        dst_ref=dst,
        send_sem=send_sem,
        recv_sem=recv_sem,
        device_id={"seq": seq, "tp": tp},
        device_id_type=MESH,
    )


def scope(name):
    return jax.named_scope(name)


def block_kernel(
    lat,
    mod,
    gains,
    wqkv,
    src_os,
    src_qkv,
    src_ot,
    src_1,
    src_2,
    result,
    xs,
    ks,
    qs,
    vs,
    ot,
    heads,
    ga,
    gm,
    mid,
    nrm,
    rows_in,
    rows_out,
    rows_back,
    tt,
    nm,
    total,
    part_out,
    part_in,
    ag_send,
    ag_recv,
    s1_send,
    s1_recv,
    own_sem,
    w_send,
    w_recv,
    d_send,
    d_recv,
    h_send,
    h_recv,
    f_send,
    f_recv,
    b_send,
    b_recv,
    m_send,
    m_recv,
):
    seq, me = lax.axis_index("seq"), lax.axis_index("tp")
    x, zh, y = seq // 8, lax.rem(seq // 4, 2), lax.rem(seq, 4)
    zl, c = me // 2, lax.rem(me, 2)
    sib = zl * 2 + (1 - c)
    unit = x * 4 + y

    def xy(dx, dy):
        return (lax.rem(x + dx + 4, 4) * 2 + zh) * 4 + lax.rem(y + dy + 4, 4)

    def zdev(dz):
        z = lax.rem(zh * 4 + zl + dz + 8, 8)
        return (x * 2 + z // 4) * 4 + y, lax.rem(z, 4) * 2 + c

    ring = (xy(1, 0), xy(-1, 0), xy(0, 1), xy(0, -1))
    peers = [(seq, lax.rem(me + i, N_TP)) for i in range(1, N_TP)]
    peers += [zdev(dz) for dz in (1, -1, 2, -2)]
    barrier = pltpu.get_barrier_semaphore()

    def signal(to_seq, to_tp):
        pl.semaphore_signal(
            barrier, inc=1, device_id={"seq": to_seq, "tp": to_tp}, device_id_type=MESH
        )

    for to_seq, to_tp in peers:
        signal(to_seq, to_tp)

    def signal_seq(i, _):
        signal(lax.rem(seq + i, N_SEQ), me)
        return 0

    lax.fori_loop(1, N_SEQ, signal_seq, 0)

    def spot(k, zs, xi, yi):
        return ga.at[zs, c, xi, yi, k] if k < ATT else gm.at[zs, xi, yi, k - ATT]

    def s1_copies(k, src):
        here = spot(k, zl, x, y)
        return [
            remote(src, here, s1_send.at[k, i], s1_recv.at[k, zl], *zdev(dz))
            for i, dz in enumerate((1, -1, 2 if k % 2 == 0 else -2))
        ]

    def s1_start(k):
        if k < ATT:
            tables = ((src_os, 0, 3), (src_qkv, 3, 12), (src_ot, 12, 16))
        else:
            tables = ((src_1, 0, 8), (src_2, 8, 16))
        for table, low, high in tables:

            @pl.when((unit >= low) & (unit < high))
            def _():
                at = jnp.clip(unit - low, 0, table.shape[0] - 1)
                src = table.at[at, k if k < ATT else k - ATT]
                pltpu.make_async_copy(src, spot(k, zl, x, y), own_sem.at[k]).start()
                for copy in s1_copies(k, src):
                    copy.start()

    def s1_wait(k):
        here = spot(k, zl, x, y)
        pltpu.make_async_copy(src_1.at[0, 0], here, own_sem.at[k]).wait()
        for i in range(1, 4):
            source = lax.rem(zl + i, 4)
            there = spot(k, source, x, y)
            remote(there, there, s1_send.at[k, 0], s1_recv.at[k, source], seq, sib).wait_recv()

    x_back, x_next = lax.rem(x + 3, 4), lax.rem(x + 1, 4)
    y_back, y_next = lax.rem(y + 3, 4), lax.rem(y + 1, 4)
    low, high = pl.ds(0, 2), pl.ds(2, 2)
    every = slice(None)

    def ring_copies(stage, k):
        if stage == 0:
            spots = [spot(k, low, x, y)] * 2 + [spot(k, high, x, y)] * 2
        elif stage == 1:
            spots = [
                spot(k, 0, x_back, y),
                spot(k, 1, x_next, y),
                spot(k, 2, x, y_back),
                spot(k, 3, x, y_next),
            ]
        elif stage == 2:
            spots = [spot(k, high, x, every)] * 2 + [spot(k, low, every, y)] * 2
        else:
            spots = [
                spot(k, 2, x_back, every),
                spot(k, 3, x_next, every),
                spot(k, 0, every, y_back),
                spot(k, 1, every, y_next),
            ]
        return [
            remote(there, there, w_send.at[stage, k, i], w_recv.at[stage, k, i], ring[i], me)
            for i, there in enumerate(spots)
        ]

    def ring_start(stage, k):
        for copy in ring_copies(stage, k):
            copy.start()

    def ring_wait(stage, k):
        for copy in ring_copies(stage, k):
            copy.wait_recv()

    def core_copy(k):
        there = ga.at[:, c, :, :, k]
        return remote(there, there, d_send.at[k], d_recv.at[k], seq, sib)

    def pump(step, k):
        with scope(f"pump_{step}_{k}"):
            if step == 0:
                s1_start(k)
            elif step == 1:
                s1_wait(k)
                ring_start(0, k)
            elif step <= 4:
                ring_wait(step - 2, k)
                ring_start(step - 1, k)
            elif step == 5:
                ring_wait(3, k)
                if k < ATT:
                    core_copy(k).start()
            else:
                core_copy(k).wait_recv()

    def ag_copy(slot, b, way):
        to = (jnp.minimum(zl + 1, 3) * 2 + c, jnp.maximum(zl - 1, 0) * 2 + c, sib)[way]
        there = xs.at[slot, b]
        return remote(there, there, ag_send.at[slot, b, way], ag_recv.at[slot, b], seq, to)

    def ag_step(distance, b, what):
        with scope(f"ag_{distance}_{b}_{what}"):
            ag_now(distance, b, what)

    def ag_now(distance, b, what):
        for way in range(2):
            origin = zl - distance if way == 0 else zl + distance
            there = (zl >= distance) if way == 0 else (zl + distance <= 3)
            more = (zl < 3) if way == 0 else (zl > 0)
            if distance == 0:
                there = more
            slot = origin * 2 + c

            @pl.when(there)
            def _():
                if what == 0 and distance > 0:
                    ag_copy(slot, b, 2).wait_recv()
                if distance == 0:
                    copy = ag_copy(slot, b, way)
                    copy.start() if what == 0 else copy.wait_send()
                else:

                    @pl.when(more)
                    def _():
                        copy = ag_copy(slot, b, way)
                        copy.start() if what == 0 else copy.wait_send()

                    copy = ag_copy(slot, b, 2)
                    copy.start() if what == 0 else copy.wait_send()

        if distance == 0:
            copy = ag_copy(me, b, 2)
            copy.start() if what == 0 else copy.wait_send()

    first_col = lax.broadcasted_iota(jnp.int32, (HW, HW), 0) == lax.broadcasted_iota(
        jnp.int32, (HW, HW), 1
    )

    def gain_column(i):
        return jnp.sum(jnp.where(first_col, gains[i : i + 1], 0.0), axis=1, keepdims=True)

    def project(z):
        with scope("project"):
            rows = xs[pl.ds(z * 2, 2)].reshape(512, D)
            queries = head_norm_rows(dot(wqkv[0], rows, 1, 1), gain_column(0)).astype(BF16)
            values = dot(wqkv[2], rows, 1, 1).astype(BF16)
            keys = head_norm_lanes(dot(rows, wqkv[1], 1, 1), gains[1:2]).astype(BF16)
            for core in range(2):
                for b in range(2):
                    at = (core * 2 + b) * 128
                    qs[b, z * 2 + core] = queries[:, at : at + 128]
                    there = pl.ds(pl.multiple_of((z * 2 + core) * 128, 128), 128)
                    vs[b, :, there] = values[:, at : at + 128]
                    ks[b, z * 2 + core] = keys[at : at + 128]

    def head_copy(b, to):
        return remote(
            ot.at[b, to], heads.at[b, me], h_send.at[b, to], h_recv.at[b, me], seq, to
        )

    def attend(b):
        with scope(f"attend_{b}"):
            attend_now(b)

    def attend_now(b):
        keys = ks[b].reshape(N_TP * 128, HW)
        values = vs[b]

        def block(i, _):
            to = lax.rem(me + 1 + i, N_TP)
            query = qs[b, to].astype(F32)
            zero = jnp.zeros((HD, 128), F32)
            pair = jnp.concatenate(
                [
                    jnp.concatenate([query[:HD], zero], axis=0),
                    jnp.concatenate([zero, query[HD:]], axis=0),
                ],
                axis=1,
            ).astype(BF16)
            weights = jnp.exp(dot(keys, pair) * SCALE)
            norm = jnp.sum(weights, axis=0, keepdims=True)
            mixed = dot(values, weights.astype(BF16)) / norm
            out = jnp.concatenate([mixed[:HD, :128], mixed[HD:, 128:]], axis=0).astype(BF16)

            @pl.when(to != me)
            def _():
                ot[b, to] = out
                head_copy(b, to).start()

            @pl.when(to == me)
            def _():
                heads[b, me] = out

            return 0

        lax.fori_loop(0, N_TP, block, 0)

    def send_rows(source, target, send, recv, b):
        def start(i, _):
            to = lax.rem(seq + i, N_SEQ)

            @pl.when((to // 16 == b) | (b < 0))
            def _():
                remote(source.at[to], target.at[seq], send.at[to], recv.at[seq], to, me).start()

            return 0

        lax.fori_loop(1, N_SEQ, start, 0)

    def take_rows(source, target, send, recv):
        target[seq] = source[seq]

        def finish(i, _):
            sender = lax.rem(seq + i, N_SEQ)
            there = target.at[sender]
            remote(there, there, send.at[sender], recv.at[sender], sender, me).wait_recv()
            return 0

        lax.fori_loop(1, N_SEQ, finish, 0)

    def drain(source, send, recv):
        def finish(i, _):
            to = lax.rem(seq + i, N_SEQ)
            there = source.at[to]
            remote(there, there, send.at[to], recv.at[to], to, me).wait_send()
            return 0

        lax.fori_loop(1, N_SEQ, finish, 0)

    def finish(b):
        with scope(f"finish_{b}"):
            for i in range(1, N_TP):
                source = lax.rem(me + i, N_TP)
                there = heads.at[b, source]
                remote(
                    there, there, h_send.at[b, source], h_recv.at[b, source], seq, source
                ).wait_recv()
            mixed = heads[b].reshape(D, 128).T
            out = dot(mixed, ga[:, :, 0, 0:3].reshape(D, D)).astype(BF16).astype(F32)
            rows = pl.ds(b * 128, 128)
            late = lat[rows].astype(F32) + mod[b, 2:3] * out
            mid[rows] = late
            normed = layer_norm(late) * (1.0 + mod[b, 4:5]) + mod[b, 3:4]
            nrm[pl.ds(b * 16, 16)] = normed.reshape(16, 8, D).astype(BF16)
            send_rows(nrm, rows_in, f_send, f_recv, b)

    def att_rows(z, core, first):
        return jnp.concatenate(
            [ga[z, core, u // 4, u % 4].reshape(48, D) for u in range(first, first + 3)], axis=0
        )

    def temporal():
        rows = rows_in[...].astype(F32).reshape(256, D).astype(BF16)
        same = lax.rem(lax.broadcasted_iota(jnp.int32, (256, 256), 0), 8) == lax.rem(
            lax.broadcasted_iota(jnp.int32, (256, 256), 1), 8
        )
        column = gain_column(2)
        zero = jnp.zeros((HD, 256), F32)

        def pair_of_heads(t, _):
            z, core = t // 2, lax.rem(t, 2)
            queries = head_norm_rows(dot(att_rows(z, core, 3), rows, 1, 1), column)
            keys = head_norm_lanes(dot(rows, att_rows(z, core, 6), 1, 1), gains[3:4]).astype(BF16)
            values = dot(att_rows(z, core, 9), rows, 1, 1).astype(BF16)
            parts = []
            for head in range(2):
                kept = queries[head * HD : (head + 1) * HD]
                kept = jnp.concatenate([kept, zero] if head == 0 else [zero, kept], axis=0)
                probs = jnp.where(same, jnp.exp(dot(keys, kept.astype(BF16)) * SCALE), 0.0)
                norm = jnp.sum(probs, axis=0, keepdims=True)
                mixed = dot(values, probs.astype(BF16)) / norm
                parts.append(mixed[head * HD : (head + 1) * HD])
            tt[t] = jnp.concatenate(parts, axis=0).astype(BF16)
            return 0

        lax.fori_loop(0, N_TP, pair_of_heads, 0)
        out = dot(tt[...].reshape(D, 256).T, ga[:, :, 3, 0:3].reshape(D, D))
        rows_out[...] = out.reshape(N_SEQ, 8, D).astype(BF16)

    def half_copy():
        return remote(nm.at[c], nm.at[c], m_send.at[0], m_recv.at[0], seq, sib)

    def part_copy():
        return remote(part_out, part_in, m_send.at[1], m_recv.at[1], seq, sib)

    def mlp_entry():
        back = rows_back[...].astype(F32).reshape(256, D)
        for b in range(2):
            rows = pl.ds(b * 128, 128)
            late = mid[rows] + mod[b, 5:6] * back[b * 128 : (b + 1) * 128]
            mid[rows] = late
            normed = layer_norm(late) * (1.0 + mod[b, 7:8]) + mod[b, 6:7]
            nm[c, rows] = normed.astype(BF16)

    def mlp_round(k, which):
        u = dot(nm[which], gm[:, 0:2, :, k].reshape(768, D), 1, 1)
        h = 0.5 * u * (1.0 + jnp.tanh(math.sqrt(2.0 / math.pi) * (u + 0.044715 * (u * u * u))))
        product = dot(h.astype(BF16), gm[:, 2:4, :, k].reshape(768, D))
        return product if k == 0 else total[which] + product

    for b in range(2):
        rows = lat[pl.ds(b * 128, 128)].astype(F32)
        xs[me, b] = (layer_norm(rows) * (1.0 + mod[b, 1:2]) + mod[b, 0:1]).astype(BF16)
    with scope("greet"):
        pl.semaphore_wait(barrier, len(peers) + N_SEQ - 1)
    pump(0, 0)
    ag_step(0, 0, 0)
    ag_step(0, 1, 0)
    pump(0, 1)
    for b in range(2):
        ag_copy(sib, b, 2).wait_recv()
    project(zl)
    pump(1, 0)
    ag_step(1, 0, 0)
    pump(1, 1)
    pump(2, 0)
    ag_step(1, 1, 0)
    pump(2, 1)
    pump(3, 0)
    ag_step(2, 0, 0)
    pump(3, 1)
    pump(0, 2)
    ag_step(2, 1, 0)
    pump(1, 2)
    ag_step(3, 0, 0)
    pump(4, 0)
    ag_step(3, 1, 0)
    pump(0, 3)
    for distance in range(1, 4):
        for b in range(2):
            other = lax.rem(zl + distance, 4) * 2 + (1 - c)
            ag_copy(other, b, 2).wait_recv()
    for i in range(1, 4):
        project(lax.rem(zl + i, 4))
    pump(2, 2)
    attend(0)
    pump(4, 1)
    pump(5, 0)
    pump(0, 4)
    attend(1)
    pump(1, 3)
    pump(3, 2)
    pump(5, 1)
    pump(6, 0)
    pump(6, 1)
    finish(0)
    finish(1)
    pump(2, 3)
    pump(1, 4)
    with scope("take_1"):
        take_rows(nrm, rows_in, f_send, f_recv)
    pump(4, 2)
    pump(3, 3)
    with scope("temporal"):
        temporal()
    send_rows(rows_out, rows_back, b_send, b_recv, -1)
    pump(2, 4)
    pump(4, 3)
    pump(3, 4)
    with scope("take_2"):
        take_rows(rows_out, rows_back, b_send, b_recv)
    with scope("entry"):
        mlp_entry()
        half_copy().start()
    pump(5, 2)
    with scope("mlp"):
        total[c] = mlp_round(0, c)
        half_copy().wait_recv()
        total[1 - c] = mlp_round(0, 1 - c)
    pump(4, 4)
    pump(5, 3)
    with scope("mlp"):
        total[c] = mlp_round(1, c)
        total[1 - c] = mlp_round(1, 1 - c)
    pump(5, 4)
    with scope("mlp"):
        part_out[...] = mlp_round(2, 1 - c).astype(BF16)
        part_copy().start()
        total[c] = mlp_round(2, c)
    with scope("last"):
        part_copy().wait_recv()
        for b in range(2):
            rows = pl.ds(b * 128, 128)
            out = (total[c, rows] + part_in[rows].astype(F32)).astype(BF16).astype(F32)
            result[rows] = (mid[rows] + mod[b, 8:9] * out).astype(BF16)

    with scope("drain"):
        half_copy().wait_send()
        part_copy().wait_send()
        drain(nrm, f_send, f_recv)
        drain(rows_out, b_send, b_recv)
        for b in range(2):
            for distance in range(4):
                ag_step(distance, b, 1)
            for i in range(1, N_TP):
                head_copy(b, lax.rem(me + i, N_TP)).wait_send()
        for k in range(ROUNDS):
            for copy in s1_copies(k, src_1.at[0, 0]):
                copy.wait_send()
            for stage in range(4):
                for copy in ring_copies(stage, k):
                    copy.wait_send()
            if k < ATT:
                core_copy(k).wait_send()


def body(
    latent,
    modulation,
    qkv_spatial,
    gain_spatial,
    out_spatial,
    qkv_temporal,
    gain_temporal,
    out_temporal,
    fc_in,
    fc_out,
):
    gains = jnp.concatenate([gain_spatial, gain_temporal], axis=0)
    gains = jnp.concatenate([gains, gains], axis=1)
    vmem = pl.BlockSpec(memory_space=pltpu.VMEM)
    hbm = pl.BlockSpec(memory_space=pl.ANY)
    dma = pltpu.SemaphoreType.DMA
    result = pl.pallas_call(
        block_kernel,
        name="block",
        out_shape=jax.ShapeDtypeStruct((256, D), BF16),
        in_specs=[vmem] * 4 + [hbm] * 5,
        out_specs=vmem,
        scratch_shapes=[
            pltpu.VMEM((N_TP, 2, 128, D), BF16),
            pltpu.VMEM((2, N_TP, 128, HW), BF16),
            pltpu.VMEM((2, N_TP, HW, 128), BF16),
            pltpu.VMEM((2, HW, 1024), BF16),
            pltpu.VMEM((2, N_TP, HW, 128), BF16),
            pltpu.VMEM((2, N_TP, HW, 128), BF16),
            pltpu.VMEM((4, 2, 4, 4, ATT, 24, D), BF16),
            pltpu.VMEM((4, 4, 4, ROUNDS - ATT, 24, D), BF16),
            pltpu.VMEM((256, D), F32),
            pltpu.VMEM((N_SEQ, 8, D), BF16),
            pltpu.VMEM((N_SEQ, 8, D), BF16),
            pltpu.VMEM((N_SEQ, 8, D), BF16),
            pltpu.VMEM((N_SEQ, 8, D), BF16),
            pltpu.VMEM((N_TP, HW, 256), BF16),
            pltpu.VMEM((2, 256, D), BF16),
            pltpu.VMEM((2, 256, D), F32),
            pltpu.VMEM((256, D), BF16),
            pltpu.VMEM((256, D), BF16),
            dma((N_TP, 2, 3)),
            dma((N_TP, 2)),
            dma((ROUNDS, 3)),
            dma((ROUNDS, 4)),
            dma((ROUNDS,)),
            dma((4, ROUNDS, 4)),
            dma((4, ROUNDS, 4)),
            dma((ATT,)),
            dma((ATT,)),
            dma((2, N_TP)),
            dma((2, N_TP)),
            dma((N_SEQ,)),
            dma((N_SEQ,)),
            dma((N_SEQ,)),
            dma((N_SEQ,)),
            dma((2,)),
            dma((2,)),
        ],
        compiler_params=pltpu.CompilerParams(
            collective_id=0, has_side_effects=True, vmem_limit_bytes=60 << 20
        ),
    )(
        latent.reshape(256, D),
        modulation,
        gains,
        qkv_spatial.transpose(0, 2, 1),
        out_spatial.reshape(3, ATT, 24, D),
        qkv_temporal.transpose(0, 2, 1).reshape(9, ATT, 24, D),
        out_temporal.reshape(3, ATT, 24, D),
        fc_in.T.reshape(8, ROUNDS - ATT, 24, D),
        fc_out.reshape(8, ROUNDS - ATT, 24, D),
    )
    return result.reshape(latent.shape)


def solution(mesh):
    placed = (
        P(None, "seq", "tp", None),
        P(),
        P(None, None, "tp"),
        P(),
        P("tp", None),
        P(None, None, "tp"),
        P(),
        P("tp", None),
        P(None, "tp"),
        P("tp", None),
    )
    return jax.shard_map(
        body, mesh=mesh, in_specs=placed, out_specs=P(None, "seq", "tp", None), check_vma=False
    )
```

time: 530 us -> 159 us (0.30)
  waiting for transfers between devices: 349 us -> 0 us
  Pallas kernels: 0 us -> 154 us
  blocking collectives: 57.2 us -> 0 us
  matrix products: 55.9 us -> 0 us
  local copies, waits for them, and re-layouts: 28.9 us -> 3.48 us
  other arithmetic: 18.6 us -> 1.43 us
  between operations: 13.8 us -> 0.01 us
    reduce_scatter x3 -> x0, waiting for transfers between devices: 176 us -> none  [body(): lax.psum_scatter(partial_value.astype(jnp.bfloat16), 'tp', scatter_dimens...]
    all_gather x3 -> x0, waiting for transfers between devices: 173 us -> none  [the longest x2 118 us: body(): lax.all_gather(normed, 'tp', axis=2, tiled=True)]
    pallas_call x0 -> x1, Pallas kernels: none -> 154 us  [body(): pl.pallas_call(block_kernel, name='block', out_shape=jax.ShapeDtypeStruct...]
    all_to_all x2 -> x0, blocking collectives: 57.2 us -> none  [the longest x1 28.6 us: body(): lax.all_to_all(normed, 'seq', split_axis=2, concat_axis=1, tiled=True)]
    dot_general x15 -> x0, matrix products: 55.9 us -> none  [the longest x6 26.8 us: project_heads(): jnp.einsum('bfpd,de->bfpe', rows_piece, table[which_part], preferred_elem...]
    convert_element_type x8 -> x0, local copies, waits for them, and re-layouts: 12.9 us -> none  [the longest x4 6.51 us: project_heads(): results.append(projected.astype(jnp.bfloat16))]
    reduce_sum x8 -> x0, other arithmetic: 8.82 us -> none  [the longest x3 3.05 us: layer_norm(): variance = jnp.mean(centred * centred, axis=-1, keepdims=True)]
    convert_element_type x8 -> x0, other arithmetic: 8.67 us -> none  [the longest x3 3.74 us: modulated(): (layer_norm(field) * (1.0 + scale_row) + shift_row).astype(jnp.bfloat16)]
  transfers between devices with their start and end apart: 6 -> 0, of which waited for: 6 -> 0; matrix products, arithmetic and copies ran while one was open for 0% -> 0% of each run, Pallas kernels for 0% -> 0%
where the time goes in v2:
time: 159 us
  Pallas kernels  154 us (97%)
  local copies, waits for them, and re-layouts  3.48 us (2%)
    pallas_call x1, Pallas kernels, body(): pl.pallas_call(block_kernel, name='block', out_shape=jax.ShapeDtypeStruct...  154 us
    unnamed x2, local copies, waits for them, and re-layouts  3.48 us

profile of v2, /device:TPU:1, one launch (start us, length us, event | category | flops | bytes accessed | tf_op | source)
XLA Modules:
  0.0 159.0 jit_solution(18090759571581262631)
XLA Ops:
  0.0 1.4 maximum_maximum_fusion.gains
  1.4 1.6 copy.11.mod
  3.0 154.1 %block.1 = bf16[256,1152]{1,0:T(8,128)(2,1)} custom-call(bf16[256,1152]{1,0:T(8,128)(2,1)} %bitcast.19, f32[2,9,1152]{2,1,0:T(8,128)} %copy.11.mod, f32[4,144]{1,0:T(4,128)} %maximum_maximum_fusion.gains, bf16[3,144,1152]{2,1,0:T(8,128)(2,1)} %bitcast.17, bf16[3,2,24,1152]{3,2,1,0:T(8,128)(2,1)} %bitcast.20, bf16[9,2,24,1152]{3,2,1,0:T(8,128)(2,1)} %bitcast.18, ...), custom_call_target="tpu_custom_call" | custom-call | tf_op jit(solution)/shard_map/block/pallas_call | solution.py:571
  157.1 1.9 %copy.14 = bf16[2,1,128,1152]{3,2,1,0:T(8,128)(2,1)} copy(bf16[2,1,128,1152]{3,2,1,0:T(8,128)(2,1)} %bitcast.14) | data formatting | bytes 1179648

commit v3 on v2

--- a/solution.py
+++ b/solution.py
@@ -73,7 +73,8 @@
 def block_kernel(
     lat,
     mod,
-    gains,
+    gain_s,
+    gain_t,
     wqkv,
     src_os,
     src_qkv,
@@ -110,10 +111,7 @@
     d_recv,
     h_send,
     h_recv,
-    f_send,
-    f_recv,
-    b_send,
-    b_recv,
+    x_sem,
     m_send,
     m_recv,
 ):
@@ -149,14 +147,18 @@
 
     lax.fori_loop(1, N_SEQ, signal_seq, 0)
 
+    def bytes_of(ref, sem):
+        pltpu.make_async_copy(ref, ref, sem).wait()
+
     def spot(k, zs, xi, yi):
         return ga.at[zs, c, xi, yi, k] if k < ATT else gm.at[zs, xi, yi, k - ATT]
 
     def s1_copies(k, src):
         here = spot(k, zl, x, y)
+        far = (zl // 2) * 4 - 2
         return [
-            remote(src, here, s1_send.at[k, i], s1_recv.at[k, zl], *zdev(dz))
-            for i, dz in enumerate((1, -1, 2 if k % 2 == 0 else -2))
+            remote(src, here, s1_send.at[k], s1_recv.at[k], *zdev(dz))
+            for dz in (1, -1, far)
         ]
 
     def s1_start(k):
@@ -177,10 +179,7 @@
     def s1_wait(k):
         here = spot(k, zl, x, y)
         pltpu.make_async_copy(src_1.at[0, 0], here, own_sem.at[k]).wait()
-        for i in range(1, 4):
-            source = lax.rem(zl + i, 4)
-            there = spot(k, source, x, y)
-            remote(there, there, s1_send.at[k, 0], s1_recv.at[k, source], seq, sib).wait_recv()
+        bytes_of(gm.at[0, 0, 0], s1_recv.at[k])
 
     x_back, x_next = lax.rem(x + 3, 4), lax.rem(x + 1, 4)
     y_back, y_next = lax.rem(y + 3, 4), lax.rem(y + 1, 4)
@@ -207,7 +206,7 @@
                 spot(k, 1, every, y_next),
             ]
         return [
-            remote(there, there, w_send.at[stage, k, i], w_recv.at[stage, k, i], ring[i], me)
+            remote(there, there, w_send.at[stage, k], w_recv.at[stage, k], ring[i], me)
             for i, there in enumerate(spots)
         ]
 
@@ -216,8 +215,12 @@
             copy.start()
 
     def ring_wait(stage, k):
-        for copy in ring_copies(stage, k):
-            copy.wait_recv()
+        bytes_of(ring_bytes(stage), w_recv.at[stage, k])
+
+    def ring_bytes(stage):
+        return (gm.at[:, 0, 0:2, 0], gm.at[:, 0, 0, 0], gm.at[:, 0:2, :, 0], gm.at[:, 0, :, 0])[
+            stage
+        ]
 
     def core_copy(k):
         there = ga.at[:, c, :, :, k]
@@ -243,66 +246,78 @@
     def ag_copy(slot, b, way):
         to = (jnp.minimum(zl + 1, 3) * 2 + c, jnp.maximum(zl - 1, 0) * 2 + c, sib)[way]
         there = xs.at[slot, b]
-        return remote(there, there, ag_send.at[slot, b, way], ag_recv.at[slot, b], seq, to)
-
-    def ag_step(distance, b, what):
-        with scope(f"ag_{distance}_{b}_{what}"):
-            ag_now(distance, b, what)
-
-    def ag_now(distance, b, what):
+        return remote(there, there, ag_send.at[way], ag_recv.at[slot, b], seq, to)
+
+    def ag_step(distance, b):
+        with scope(f"ag_{distance}_{b}"):
+            ag_now(distance, b)
+
+    def ag_now(distance, b):
         for way in range(2):
             origin = zl - distance if way == 0 else zl + distance
             there = (zl >= distance) if way == 0 else (zl + distance <= 3)
             more = (zl < 3) if way == 0 else (zl > 0)
-            if distance == 0:
-                there = more
             slot = origin * 2 + c
 
             @pl.when(there)
             def _():
-                if what == 0 and distance > 0:
+                if distance > 0:
                     ag_copy(slot, b, 2).wait_recv()
-                if distance == 0:
-                    copy = ag_copy(slot, b, way)
-                    copy.start() if what == 0 else copy.wait_send()
-                else:
-
-                    @pl.when(more)
-                    def _():
-                        copy = ag_copy(slot, b, way)
-                        copy.start() if what == 0 else copy.wait_send()
-
-                    copy = ag_copy(slot, b, 2)
-                    copy.start() if what == 0 else copy.wait_send()
-
-        if distance == 0:
-            copy = ag_copy(me, b, 2)
-            copy.start() if what == 0 else copy.wait_send()
-
-    first_col = lax.broadcasted_iota(jnp.int32, (HW, HW), 0) == lax.broadcasted_iota(
-        jnp.int32, (HW, HW), 1
-    )
-
-    def gain_column(i):
-        return jnp.sum(jnp.where(first_col, gains[i : i + 1], 0.0), axis=1, keepdims=True)
-
-    def project(z):
+
+                @pl.when(more)
+                def _():
+                    ag_copy(slot, b, way).start()
+
+                if distance > 0 or way == 0:
+                    ag_copy(slot, b, 2).start()
+
+    def ag_drain():
+        bytes_of(xs.at[0:4], ag_send.at[2])
+        for z in range(4):
+
+            @pl.when(zl == z)
+            def _():
+                if z < 3:
+                    bytes_of(xs.at[0 : z + 1], ag_send.at[0])
+                if z > 0:
+                    bytes_of(xs.at[0 : 4 - z], ag_send.at[1])
+
+    def diagonal(n):
+        return lax.broadcasted_iota(jnp.int32, (n, n), 0) == lax.broadcasted_iota(
+            jnp.int32, (n, n), 1
+        )
+
+    def gain_column(gains, i):
+        column = jnp.where(diagonal(HD), gains[i : i + 1], 0.0)
+        column = jnp.sum(column, axis=1, keepdims=True)
+        return jnp.concatenate([column, column], axis=0)
+
+    def gain_row(gains, i):
+        return jnp.sum(
+            jnp.where(diagonal(HW), gain_column(gains, i), 0.0), axis=0, keepdims=True
+        )
+
+    query_gain, key_gain = gain_column(gain_s, 0), gain_row(gain_s, 1)
+
+    def project(z, b):
         with scope("project"):
-            rows = xs[pl.ds(z * 2, 2)].reshape(512, D)
-            queries = head_norm_rows(dot(wqkv[0], rows, 1, 1), gain_column(0)).astype(BF16)
+            rows = xs[pl.ds(z * 2, 2), b].reshape(256, D)
+            queries = head_norm_rows(dot(wqkv[0], rows, 1, 1), query_gain).astype(BF16)
             values = dot(wqkv[2], rows, 1, 1).astype(BF16)
-            keys = head_norm_lanes(dot(rows, wqkv[1], 1, 1), gains[1:2]).astype(BF16)
+            keys = head_norm_lanes(dot(rows, wqkv[1], 1, 1), key_gain).astype(BF16)
             for core in range(2):
-                for b in range(2):
-                    at = (core * 2 + b) * 128
-                    qs[b, z * 2 + core] = queries[:, at : at + 128]
-                    there = pl.ds(pl.multiple_of((z * 2 + core) * 128, 128), 128)
-                    vs[b, :, there] = values[:, at : at + 128]
-                    ks[b, z * 2 + core] = keys[at : at + 128]
+                at = core * 128
+                qs[b, z * 2 + core] = queries[:, at : at + 128]
+                there = pl.ds(pl.multiple_of((z * 2 + core) * 128, 128), 128)
+                vs[b, :, there] = values[:, at : at + 128]
+                ks[b, z * 2 + core] = keys[at : at + 128]
+
+    def take_core(z, b):
+        ag_copy(z * 2 + (1 - c), b, 2).wait_recv()
 
     def head_copy(b, to):
         return remote(
-            ot.at[b, to], heads.at[b, me], h_send.at[b, to], h_recv.at[b, me], seq, to
+            ot.at[b, to], heads.at[b, me], h_send.at[b], h_recv.at[b], seq, to
         )
 
     def attend(b):
@@ -348,66 +363,45 @@
 
             @pl.when((to // 16 == b) | (b < 0))
             def _():
-                remote(source.at[to], target.at[seq], send.at[to], recv.at[seq], to, me).start()
+                remote(source.at[to], target.at[seq], send, recv, to, me).start()
 
             return 0
 
         lax.fori_loop(1, N_SEQ, start, 0)
 
-    def take_rows(source, target, send, recv):
+    def take_rows(source, target, recv):
         target[seq] = source[seq]
-
-        def finish(i, _):
-            sender = lax.rem(seq + i, N_SEQ)
-            there = target.at[sender]
-            remote(there, there, send.at[sender], recv.at[sender], sender, me).wait_recv()
-            return 0
-
-        lax.fori_loop(1, N_SEQ, finish, 0)
-
-    def drain(source, send, recv):
-        def finish(i, _):
-            to = lax.rem(seq + i, N_SEQ)
-            there = source.at[to]
-            remote(there, there, send.at[to], recv.at[to], to, me).wait_send()
-            return 0
-
-        lax.fori_loop(1, N_SEQ, finish, 0)
+        bytes_of(target.at[0:31], recv)
 
     def finish(b):
         with scope(f"finish_{b}"):
-            for i in range(1, N_TP):
-                source = lax.rem(me + i, N_TP)
-                there = heads.at[b, source]
-                remote(
-                    there, there, h_send.at[b, source], h_recv.at[b, source], seq, source
-                ).wait_recv()
+            bytes_of(heads.at[b, 0:7], h_recv.at[b])
             mixed = heads[b].reshape(D, 128).T
             out = dot(mixed, ga[:, :, 0, 0:3].reshape(D, D)).astype(BF16).astype(F32)
             rows = pl.ds(b * 128, 128)
-            late = lat[rows].astype(F32) + mod[b, 2:3] * out
+            late = lat[rows].astype(F32) + mod[2, b : b + 1] * out
             mid[rows] = late
-            normed = layer_norm(late) * (1.0 + mod[b, 4:5]) + mod[b, 3:4]
+            normed = layer_norm(late) * (1.0 + mod[4, b : b + 1]) + mod[3, b : b + 1]
             nrm[pl.ds(b * 16, 16)] = normed.reshape(16, 8, D).astype(BF16)
-            send_rows(nrm, rows_in, f_send, f_recv, b)
+            send_rows(nrm, rows_in, x_sem.at[0], x_sem.at[1], b)
 
     def att_rows(z, core, first):
         return jnp.concatenate(
             [ga[z, core, u // 4, u % 4].reshape(48, D) for u in range(first, first + 3)], axis=0
         )
 
-    def temporal():
+    def temporal(half):
         rows = rows_in[...].astype(F32).reshape(256, D).astype(BF16)
         same = lax.rem(lax.broadcasted_iota(jnp.int32, (256, 256), 0), 8) == lax.rem(
             lax.broadcasted_iota(jnp.int32, (256, 256), 1), 8
         )
-        column = gain_column(2)
+        column, row = gain_column(gain_t, 0), gain_row(gain_t, 1)
         zero = jnp.zeros((HD, 256), F32)
 
         def pair_of_heads(t, _):
             z, core = t // 2, lax.rem(t, 2)
             queries = head_norm_rows(dot(att_rows(z, core, 3), rows, 1, 1), column)
-            keys = head_norm_lanes(dot(rows, att_rows(z, core, 6), 1, 1), gains[3:4]).astype(BF16)
+            keys = head_norm_lanes(dot(rows, att_rows(z, core, 6), 1, 1), row).astype(BF16)
             values = dot(att_rows(z, core, 9), rows, 1, 1).astype(BF16)
             parts = []
             for head in range(2):
@@ -420,7 +414,9 @@
             tt[t] = jnp.concatenate(parts, axis=0).astype(BF16)
             return 0
 
-        lax.fori_loop(0, N_TP, pair_of_heads, 0)
+        lax.fori_loop(half * 4, half * 4 + 4, pair_of_heads, 0)
+        if half == 0:
+            return
         out = dot(tt[...].reshape(D, 256).T, ga[:, :, 3, 0:3].reshape(D, D))
         rows_out[...] = out.reshape(N_SEQ, 8, D).astype(BF16)
 
@@ -434,9 +430,9 @@
         back = rows_back[...].astype(F32).reshape(256, D)
         for b in range(2):
             rows = pl.ds(b * 128, 128)
-            late = mid[rows] + mod[b, 5:6] * back[b * 128 : (b + 1) * 128]
+            late = mid[rows] + mod[5, b : b + 1] * back[b * 128 : (b + 1) * 128]
             mid[rows] = late
-            normed = layer_norm(late) * (1.0 + mod[b, 7:8]) + mod[b, 6:7]
+            normed = layer_norm(late) * (1.0 + mod[7, b : b + 1]) + mod[6, b : b + 1]
             nm[c, rows] = normed.astype(BF16)
 
     def mlp_round(k, which):
@@ -447,75 +443,86 @@
 
     for b in range(2):
         rows = lat[pl.ds(b * 128, 128)].astype(F32)
-        xs[me, b] = (layer_norm(rows) * (1.0 + mod[b, 1:2]) + mod[b, 0:1]).astype(BF16)
+        xs[me, b] = (layer_norm(rows) * (1.0 + mod[1, b : b + 1]) + mod[0, b : b + 1]).astype(BF16)
     with scope("greet"):
         pl.semaphore_wait(barrier, len(peers) + N_SEQ - 1)
+    near = zl + 1 - 2 * lax.rem(zl, 2)
+    middle = 2 - zl // 2
+    far = 3 - 3 * (zl // 2)
     pump(0, 0)
-    ag_step(0, 0, 0)
-    ag_step(0, 1, 0)
     pump(0, 1)
+    ag_step(0, 0)
+    ag_step(0, 1)
     for b in range(2):
-        ag_copy(sib, b, 2).wait_recv()
-    project(zl)
+        take_core(zl, b)
+        project(zl, b)
     pump(1, 0)
-    ag_step(1, 0, 0)
     pump(1, 1)
     pump(2, 0)
-    ag_step(1, 1, 0)
     pump(2, 1)
     pump(3, 0)
-    ag_step(2, 0, 0)
+    ag_step(1, 0)
     pump(3, 1)
+    take_core(near, 0)
+    project(near, 0)
+    ag_step(1, 1)
+    take_core(near, 1)
+    project(near, 1)
     pump(0, 2)
-    ag_step(2, 1, 0)
+    ag_step(2, 0)
+    take_core(middle, 0)
+    project(middle, 0)
+    ag_step(2, 1)
+    take_core(middle, 1)
+    project(middle, 1)
+    pump(4, 0)
     pump(1, 2)
-    ag_step(3, 0, 0)
-    pump(4, 0)
-    ag_step(3, 1, 0)
     pump(0, 3)
-    for distance in range(1, 4):
-        for b in range(2):
-            other = lax.rem(zl + distance, 4) * 2 + (1 - c)
-            ag_copy(other, b, 2).wait_recv()
-    for i in range(1, 4):
-        project(lax.rem(zl + i, 4))
+    ag_step(3, 0)
+    take_core(far, 0)
+    project(far, 0)
+    pump(4, 1)
+    attend(0)
     pump(2, 2)
-    attend(0)
-    pump(4, 1)
     pump(5, 0)
+    pump(1, 3)
+    ag_step(3, 1)
+    take_core(far, 1)
+    project(far, 1)
+    pump(3, 2)
     pump(0, 4)
     attend(1)
-    pump(1, 3)
-    pump(3, 2)
     pump(5, 1)
+    pump(2, 3)
     pump(6, 0)
     pump(6, 1)
     finish(0)
     finish(1)
-    pump(2, 3)
+    pump(3, 3)
     pump(1, 4)
+    pump(4, 2)
     with scope("take_1"):
-        take_rows(nrm, rows_in, f_send, f_recv)
-    pump(4, 2)
-    pump(3, 3)
+        take_rows(nrm, rows_in, x_sem.at[1])
     with scope("temporal"):
-        temporal()
-    send_rows(rows_out, rows_back, b_send, b_recv, -1)
+        temporal(0)
     pump(2, 4)
+    with scope("temporal"):
+        temporal(1)
+    send_rows(rows_out, rows_back, x_sem.at[2], x_sem.at[3], -1)
     pump(4, 3)
     pump(3, 4)
+    pump(5, 2)
     with scope("take_2"):
-        take_rows(rows_out, rows_back, b_send, b_recv)
+        take_rows(rows_out, rows_back, x_sem.at[3])
     with scope("entry"):
         mlp_entry()
         half_copy().start()
-    pump(5, 2)
     with scope("mlp"):
         total[c] = mlp_round(0, c)
         half_copy().wait_recv()
         total[1 - c] = mlp_round(0, 1 - c)
+    pump(5, 3)
     pump(4, 4)
-    pump(5, 3)
     with scope("mlp"):
         total[c] = mlp_round(1, c)
         total[1 - c] = mlp_round(1, 1 - c)
@@ -529,24 +536,20 @@
         for b in range(2):
             rows = pl.ds(b * 128, 128)
             out = (total[c, rows] + part_in[rows].astype(F32)).astype(BF16).astype(F32)
-            result[rows] = (mid[rows] + mod[b, 8:9] * out).astype(BF16)
+            result[rows] = (mid[rows] + mod[8, b : b + 1] * out).astype(BF16)
 
     with scope("drain"):
         half_copy().wait_send()
         part_copy().wait_send()
-        drain(nrm, f_send, f_recv)
-        drain(rows_out, b_send, b_recv)
+        bytes_of(nrm.at[0:31], x_sem.at[0])
+        bytes_of(rows_out.at[0:31], x_sem.at[2])
+        ag_drain()
         for b in range(2):
-            for distance in range(4):
-                ag_step(distance, b, 1)
-            for i in range(1, N_TP):
-                head_copy(b, lax.rem(me + i, N_TP)).wait_send()
+            bytes_of(ot.at[b, 0:7], h_send.at[b])
         for k in range(ROUNDS):
-            for copy in s1_copies(k, src_1.at[0, 0]):
-                copy.wait_send()
+            bytes_of(gm.at[0, 0, 0], s1_send.at[k])
             for stage in range(4):
-                for copy in ring_copies(stage, k):
-                    copy.wait_send()
+                bytes_of(ring_bytes(stage), w_send.at[stage, k])
             if k < ATT:
                 core_copy(k).wait_send()
 
@@ -563,8 +566,6 @@
     fc_in,
     fc_out,
 ):
-    gains = jnp.concatenate([gain_spatial, gain_temporal], axis=0)
-    gains = jnp.concatenate([gains, gains], axis=1)
     vmem = pl.BlockSpec(memory_space=pltpu.VMEM)
     hbm = pl.BlockSpec(memory_space=pl.ANY)
     dma = pltpu.SemaphoreType.DMA
@@ -572,7 +573,7 @@
         block_kernel,
         name="block",
         out_shape=jax.ShapeDtypeStruct((256, D), BF16),
-        in_specs=[vmem] * 4 + [hbm] * 5,
+        in_specs=[vmem] * 5 + [hbm] * 5,
         out_specs=vmem,
         scratch_shapes=[
             pltpu.VMEM((N_TP, 2, 128, D), BF16),
@@ -593,21 +594,18 @@
             pltpu.VMEM((2, 256, D), F32),
             pltpu.VMEM((256, D), BF16),
             pltpu.VMEM((256, D), BF16),
-            dma((N_TP, 2, 3)),
+            dma((3,)),
             dma((N_TP, 2)),
-            dma((ROUNDS, 3)),
-            dma((ROUNDS, 4)),
             dma((ROUNDS,)),
-            dma((4, ROUNDS, 4)),
-            dma((4, ROUNDS, 4)),
+            dma((ROUNDS,)),
+            dma((ROUNDS,)),
+            dma((4, ROUNDS)),
+            dma((4, ROUNDS)),
             dma((ATT,)),
             dma((ATT,)),
-            dma((2, N_TP)),
-            dma((2, N_TP)),
-            dma((N_SEQ,)),
-            dma((N_SEQ,)),
-            dma((N_SEQ,)),
-            dma((N_SEQ,)),
+            dma((2,)),
+            dma((2,)),
+            dma((4,)),
             dma((2,)),
             dma((2,)),
         ],
@@ -616,8 +614,9 @@
         ),
     )(
         latent.reshape(256, D),
-        modulation,
-        gains,
+        modulation.transpose(1, 0, 2),
+        gain_spatial,
+        gain_temporal,
         qkv_spatial.transpose(0, 2, 1),
         out_spatial.reshape(3, ATT, 24, D),
         qkv_temporal.transpose(0, 2, 1).reshape(9, ATT, 24, D),

time: 159 us -> 148 us (0.931)
  Pallas kernels: 154 us -> 146 us
    pallas_call x1, Pallas kernels: 154 us -> 146 us  [body(): pl.pallas_call(block_kernel, name='block', out_shape=jax.ShapeDtypeStruct...]
    unnamed x2 -> x1, local copies, waits for them, and re-layouts: 3.48 us -> 1.92 us
where the time goes in v3:
time: 148 us
  Pallas kernels  146 us (99%)
  local copies, waits for them, and re-layouts  1.92 us (1%)
    pallas_call x1, Pallas kernels, body(): pl.pallas_call(block_kernel, name='block', out_shape=jax.ShapeDtypeStruct...  146 us

profile of v3, /device:TPU:1, one launch (start us, length us, event | category | flops | bytes accessed | tf_op | source)
XLA Modules:
  0.0 148.3 jit_solution(16448015515202595955)
XLA Ops:
  0.0 146.3 %block.1 = bf16[256,1152]{1,0:T(8,128)(2,1)} custom-call(bf16[256,1152]{1,0:T(8,128)(2,1)} %bitcast.20, f32[9,2,1152]{2,1,0:T(2,128)} %bitcast.23, f32[2,72]{1,0:T(2,128)} %gain_s.1, f32[2,72]{1,0:T(2,128)} %gain_t.1, bf16[3,144,1152]{2,1,0:T(8,128)(2,1)} %bitcast.18, bf16[3,2,24,1152]{3,2,1,0:T(8,128)(2,1)} %bitcast.21, bf16[9,2,24,1152]{3,2,1,0:T(8,128)(2,1)} %bitcast.19, ...), custom_call_target="tpu_custom_call" | custom-call | tf_op jit(solution)/shard_map/block/pallas_call | solution.py:572
  146.3 1.9 %copy.13 = bf16[2,1,128,1152]{3,2,1,0:T(8,128)(2,1)} copy(bf16[2,1,128,1152]{3,2,1,0:T(8,128)(2,1)} %bitcast.15) | data formatting | bytes 1179648

commit v4 on v3

--- a/solution.py
+++ b/solution.py
@@ -21,6 +21,7 @@
 
 ATT = 2
 ROUNDS = 5
+WIDE = ()
 
 
 def layer_norm(values):
@@ -153,15 +154,16 @@
     def spot(k, zs, xi, yi):
         return ga.at[zs, c, xi, yi, k] if k < ATT else gm.at[zs, xi, yi, k - ATT]
 
-    def s1_copies(k, src):
-        here = spot(k, zl, x, y)
-        far = (zl // 2) * 4 - 2
-        return [
-            remote(src, here, s1_send.at[k], s1_recv.at[k], *zdev(dz))
-            for dz in (1, -1, far)
-        ]
+    far_z = (zl // 2) * 4 - 2
+
+    def s1_send_to_all(k, src, dst):
+        pltpu.make_async_copy(src, dst, own_sem.at[k]).start()
+        for dz in (1, -1, far_z):
+            remote(src, dst, s1_send.at[k], s1_recv.at[k], *zdev(dz)).start()
 
     def s1_start(k):
+        if k in WIDE:
+            return s1_start_wide(k)
         if k < ATT:
             tables = ((src_os, 0, 3), (src_qkv, 3, 12), (src_ot, 12, 16))
         else:
@@ -170,16 +172,32 @@
 
             @pl.when((unit >= low) & (unit < high))
             def _():
-                at = jnp.clip(unit - low, 0, table.shape[0] - 1)
-                src = table.at[at, k if k < ATT else k - ATT]
-                pltpu.make_async_copy(src, spot(k, zl, x, y), own_sem.at[k]).start()
-                for copy in s1_copies(k, src):
-                    copy.start()
+                if k < ATT:
+                    src = table.at[jnp.clip(unit - low, 0, table.shape[0] - 1), k]
+                else:
+                    src = table.at[lax.rem(x, 2), y, k - ATT]
+                s1_send_to_all(k, src, spot(k, zl, x, y))
+
+    def s1_start_wide(k):
+        j = k - ATT
+
+        @pl.when(zl < 2)
+        def _():
+            s1_send_to_all(k, src_1.at[:, y, j], gm.at[zl, 0:2, y, j])
+            s1_send_to_all(k, src_2.at[:, y, j], gm.at[zl, 2:4, y, j])
+
+        for table, first in ((src_1, 0), (src_2, 2)):
+
+            @pl.when((zl >= 2) & (x // 2 == first // 2))
+            def _():
+                s1_send_to_all(k, table.at[lax.rem(x, 2), :, j], gm.at[zl, x, :, j])
+
+    def s1_bytes(k):
+        return gm.at[0:3, 0, :, 0] if k in WIDE else gm.at[0, 0, 0]
 
     def s1_wait(k):
-        here = spot(k, zl, x, y)
-        pltpu.make_async_copy(src_1.at[0, 0], here, own_sem.at[k]).wait()
-        bytes_of(gm.at[0, 0, 0], s1_recv.at[k])
+        bytes_of(gm.at[0, 0, :, 0] if k in WIDE else gm.at[0, 0, 0, 0], own_sem.at[k])
+        bytes_of(s1_bytes(k), s1_recv.at[k])
 
     x_back, x_next = lax.rem(x + 3, 4), lax.rem(x + 1, 4)
     y_back, y_next = lax.rem(y + 3, 4), lax.rem(y + 1, 4)
@@ -232,7 +250,7 @@
                 s1_start(k)
             elif step == 1:
                 s1_wait(k)
-                ring_start(0, k)
+                ring_start(2 if k in WIDE else 0, k)
             elif step <= 4:
                 ring_wait(step - 2, k)
                 ring_start(step - 1, k)
@@ -320,15 +338,15 @@
             ot.at[b, to], heads.at[b, me], h_send.at[b], h_recv.at[b], seq, to
         )
 
-    def attend(b):
-        with scope(f"attend_{b}"):
-            attend_now(b)
-
-    def attend_now(b):
+    def attend(b, half):
+        with scope(f"attend_{b}_{half}"):
+            attend_now(b, half)
+
+    def attend_now(b, half):
         keys = ks[b].reshape(N_TP * 128, HW)
         values = vs[b]
 
-        def block(i, _):
+        def block(i):
             to = lax.rem(me + 1 + i, N_TP)
             query = qs[b, to].astype(F32)
             zero = jnp.zeros((HD, 128), F32)
@@ -353,9 +371,11 @@
             def _():
                 heads[b, me] = out
 
+        def one_block(i, _):
+            block(i)
             return 0
 
-        lax.fori_loop(0, N_TP, block, 0)
+        lax.fori_loop(half * 4, half * 4 + 4, one_block, 0)
 
     def send_rows(source, target, send, recv, b):
         def start(i, _):
@@ -398,7 +418,7 @@
         column, row = gain_column(gain_t, 0), gain_row(gain_t, 1)
         zero = jnp.zeros((HD, 256), F32)
 
-        def pair_of_heads(t, _):
+        def pair_of_heads(t):
             z, core = t // 2, lax.rem(t, 2)
             queries = head_norm_rows(dot(att_rows(z, core, 3), rows, 1, 1), column)
             keys = head_norm_lanes(dot(rows, att_rows(z, core, 6), 1, 1), row).astype(BF16)
@@ -411,10 +431,15 @@
                 norm = jnp.sum(probs, axis=0, keepdims=True)
                 mixed = dot(values, probs.astype(BF16)) / norm
                 parts.append(mixed[head * HD : (head + 1) * HD])
-            tt[t] = jnp.concatenate(parts, axis=0).astype(BF16)
+            return jnp.concatenate(parts, axis=0).astype(BF16)
+
+        def two_pairs(i, _):
+            first, second = pair_of_heads(2 * i), pair_of_heads(2 * i + 1)
+            tt[2 * i] = first
+            tt[2 * i + 1] = second
             return 0
 
-        lax.fori_loop(half * 4, half * 4 + 4, pair_of_heads, 0)
+        lax.fori_loop(half * 2, half * 2 + 2, two_pairs, 0)
         if half == 0:
             return
         out = dot(tt[...].reshape(D, 256).T, ga[:, :, 3, 0:3].reshape(D, D))
@@ -461,6 +486,7 @@
     pump(2, 0)
     pump(2, 1)
     pump(3, 0)
+    pump(0, 2)
     ag_step(1, 0)
     pump(3, 1)
     take_core(near, 0)
@@ -468,39 +494,40 @@
     ag_step(1, 1)
     take_core(near, 1)
     project(near, 1)
-    pump(0, 2)
+    pump(0, 3)
     ag_step(2, 0)
+    pump(4, 0)
     take_core(middle, 0)
     project(middle, 0)
+    pump(1, 2)
     ag_step(2, 1)
     take_core(middle, 1)
     project(middle, 1)
-    pump(4, 0)
-    pump(1, 2)
-    pump(0, 3)
+    pump(4, 1)
+    pump(1, 3)
+    pump(2, 2)
     ag_step(3, 0)
     take_core(far, 0)
+    pump(5, 0)
     project(far, 0)
-    pump(4, 1)
-    attend(0)
-    pump(2, 2)
-    pump(5, 0)
-    pump(1, 3)
+    attend(0, 0)
+    pump(3, 2)
+    attend(0, 1)
+    pump(2, 3)
     ag_step(3, 1)
     take_core(far, 1)
+    pump(5, 1)
+    pump(0, 4)
     project(far, 1)
-    pump(3, 2)
-    pump(0, 4)
-    attend(1)
-    pump(5, 1)
-    pump(2, 3)
+    attend(1, 0)
+    attend(1, 1)
+    pump(4, 2)
     pump(6, 0)
     pump(6, 1)
     finish(0)
     finish(1)
+    pump(1, 4)
     pump(3, 3)
-    pump(1, 4)
-    pump(4, 2)
     with scope("take_1"):
         take_rows(nrm, rows_in, x_sem.at[1])
     with scope("temporal"):
@@ -509,8 +536,8 @@
     with scope("temporal"):
         temporal(1)
     send_rows(rows_out, rows_back, x_sem.at[2], x_sem.at[3], -1)
+    pump(3, 4)
     pump(4, 3)
-    pump(3, 4)
     pump(5, 2)
     with scope("take_2"):
         take_rows(rows_out, rows_back, x_sem.at[3])
@@ -521,8 +548,8 @@
         total[c] = mlp_round(0, c)
         half_copy().wait_recv()
         total[1 - c] = mlp_round(0, 1 - c)
+    pump(4, 4)
     pump(5, 3)
-    pump(4, 4)
     with scope("mlp"):
         total[c] = mlp_round(1, c)
         total[1 - c] = mlp_round(1, 1 - c)
@@ -547,8 +574,8 @@
         for b in range(2):
             bytes_of(ot.at[b, 0:7], h_send.at[b])
         for k in range(ROUNDS):
-            bytes_of(gm.at[0, 0, 0], s1_send.at[k])
-            for stage in range(4):
+            bytes_of(s1_bytes(k), s1_send.at[k])
+            for stage in range(2 if k in WIDE else 0, 4):
                 bytes_of(ring_bytes(stage), w_send.at[stage, k])
             if k < ATT:
                 core_copy(k).wait_send()
@@ -610,7 +637,7 @@
             dma((2,)),
         ],
         compiler_params=pltpu.CompilerParams(
-            collective_id=0, has_side_effects=True, vmem_limit_bytes=60 << 20
+            collective_id=0, has_side_effects=True, vmem_limit_bytes=54 << 20
         ),
     )(
         latent.reshape(256, D),
@@ -621,8 +648,8 @@
         out_spatial.reshape(3, ATT, 24, D),
         qkv_temporal.transpose(0, 2, 1).reshape(9, ATT, 24, D),
         out_temporal.reshape(3, ATT, 24, D),
-        fc_in.T.reshape(8, ROUNDS - ATT, 24, D),
-        fc_out.reshape(8, ROUNDS - ATT, 24, D),
+        fc_in.T.reshape(2, 4, ROUNDS - ATT, 24, D),
+        fc_out.reshape(2, 4, ROUNDS - ATT, 24, D),
     )
     return result.reshape(latent.shape)
 

time: 148 us -> 142 us (0.959)
  the two profiles are of different devices: /device:TPU:1 before, /device:TPU:121 now
where the time goes in v4:
time: 142 us
  Pallas kernels  140 us (99%)
  local copies, waits for them, and re-layouts  1.92 us (1%)
    pallas_call x1, Pallas kernels, body(): pl.pallas_call(block_kernel, name='block', out_shape=jax.ShapeDtypeStruct...  140 us

profile of v4, /device:TPU:121, one launch (start us, length us, event | category | flops | bytes accessed | tf_op | source)
XLA Modules:
  0.0 142.2 jit_solution(17038056659701417421)
XLA Ops:
  0.0 140.2 %block.1 = bf16[256,1152]{1,0:T(8,128)(2,1)} custom-call(bf16[256,1152]{1,0:T(8,128)(2,1)} %bitcast.20, f32[9,2,1152]{2,1,0:T(2,128)} %bitcast.23, f32[2,72]{1,0:T(2,128)} %gain_s.1, f32[2,72]{1,0:T(2,128)} %gain_t.1, bf16[3,144,1152]{2,1,0:T(8,128)(2,1)} %bitcast.18, bf16[3,2,24,1152]{3,2,1,0:T(8,128)(2,1)} %bitcast.21, bf16[9,2,24,1152]{3,2,1,0:T(8,128)(2,1)} %bitcast.19, ...), custom_call_target="tpu_custom_call" | custom-call | tf_op jit(solution)/shard_map/block/pallas_call | solution.py:599
  140.2 1.9 %copy.13 = bf16[2,1,128,1152]{3,2,1,0:T(8,128)(2,1)} copy(bf16[2,1,128,1152]{3,2,1,0:T(8,128)(2,1)} %bitcast.15) | data formatting | bytes 1179648

commit v5 on v4

--- a/solution.py
+++ b/solution.py
@@ -20,8 +20,8 @@
 BF16 = jnp.bfloat16
 
 ATT = 2
-ROUNDS = 5
-WIDE = ()
+MLP_ROWS = (32, 32, 8)
+ROUNDS = ATT + len(MLP_ROWS)
 
 
 def layer_norm(values):
@@ -72,17 +72,21 @@
 
 
 def block_kernel(
-    lat,
-    mod,
+    lat_in,
+    mod_in,
     gain_s,
     gain_t,
-    wqkv,
+    wqkv_in,
     src_os,
     src_qkv,
     src_ot,
     src_1,
     src_2,
     result,
+    lat,
+    mod,
+    wqkv,
+    in_sem,
     xs,
     ks,
     qs,
@@ -90,7 +94,9 @@
     ot,
     heads,
     ga,
-    gm,
+    gm0,
+    gm1,
+    gm2,
     mid,
     nrm,
     rows_in,
@@ -141,6 +147,12 @@
 
     for to_seq, to_tp in peers:
         signal(to_seq, to_tp)
+    loads = [
+        pltpu.make_async_copy(src, dst, in_sem.at[i])
+        for i, (src, dst) in enumerate(((lat_in, lat), (mod_in, mod), (wqkv_in, wqkv)))
+    ]
+    for load in loads:
+        load.start()
 
     def signal_seq(i, _):
         signal(lax.rem(seq + i, N_SEQ), me)
@@ -151,52 +163,37 @@
     def bytes_of(ref, sem):
         pltpu.make_async_copy(ref, ref, sem).wait()
 
-    def spot(k, zs, xi, yi):
-        return ga.at[zs, c, xi, yi, k] if k < ATT else gm.at[zs, xi, yi, k - ATT]
+    gm = (gm0, gm1, gm2)
+
+    def spot(k, zs, xi, yi, core=c):
+        return ga.at[zs, core, xi, yi, k] if k < ATT else gm[k - ATT].at[zs, xi, yi]
 
     far_z = (zl // 2) * 4 - 2
 
-    def s1_send_to_all(k, src, dst):
-        pltpu.make_async_copy(src, dst, own_sem.at[k]).start()
-        for dz in (1, -1, far_z):
-            remote(src, dst, s1_send.at[k], s1_recv.at[k], *zdev(dz)).start()
-
     def s1_start(k):
-        if k in WIDE:
-            return s1_start_wide(k)
         if k < ATT:
             tables = ((src_os, 0, 3), (src_qkv, 3, 12), (src_ot, 12, 16))
         else:
             tables = ((src_1, 0, 8), (src_2, 8, 16))
-        for table, low, high in tables:
-
-            @pl.when((unit >= low) & (unit < high))
+        for table, first, last in tables:
+
+            @pl.when((unit >= first) & (unit < last))
             def _():
                 if k < ATT:
-                    src = table.at[jnp.clip(unit - low, 0, table.shape[0] - 1), k]
+                    src = table.at[jnp.clip(unit - first, 0, table.shape[0] - 1), k]
                 else:
-                    src = table.at[lax.rem(x, 2), y, k - ATT]
-                s1_send_to_all(k, src, spot(k, zl, x, y))
-
-    def s1_start_wide(k):
-        j = k - ATT
-
-        @pl.when(zl < 2)
-        def _():
-            s1_send_to_all(k, src_1.at[:, y, j], gm.at[zl, 0:2, y, j])
-            s1_send_to_all(k, src_2.at[:, y, j], gm.at[zl, 2:4, y, j])
-
-        for table, first in ((src_1, 0), (src_2, 2)):
-
-            @pl.when((zl >= 2) & (x // 2 == first // 2))
-            def _():
-                s1_send_to_all(k, table.at[lax.rem(x, 2), :, j], gm.at[zl, x, :, j])
+                    rows = pl.ds(sum(MLP_ROWS[: k - ATT]), MLP_ROWS[k - ATT])
+                    src = table.at[lax.rem(x, 2), y, rows]
+                dst = spot(k, zl, x, y)
+                pltpu.make_async_copy(src, dst, own_sem.at[k]).start()
+                for dz in (1, -1, far_z):
+                    remote(src, dst, s1_send.at[k], s1_recv.at[k], *zdev(dz)).start()
 
     def s1_bytes(k):
-        return gm.at[0:3, 0, :, 0] if k in WIDE else gm.at[0, 0, 0]
+        return spot(k, slice(0, 3), 0, 0, 0)
 
     def s1_wait(k):
-        bytes_of(gm.at[0, 0, :, 0] if k in WIDE else gm.at[0, 0, 0, 0], own_sem.at[k])
+        bytes_of(spot(k, 0, 0, 0, 0), own_sem.at[k])
         bytes_of(s1_bytes(k), s1_recv.at[k])
 
     x_back, x_next = lax.rem(x + 3, 4), lax.rem(x + 1, 4)
@@ -233,16 +230,23 @@
             copy.start()
 
     def ring_wait(stage, k):
-        bytes_of(ring_bytes(stage), w_recv.at[stage, k])
-
-    def ring_bytes(stage):
-        return (gm.at[:, 0, 0:2, 0], gm.at[:, 0, 0, 0], gm.at[:, 0:2, :, 0], gm.at[:, 0, :, 0])[
-            stage
-        ]
-
-    def core_copy(k):
-        there = ga.at[:, c, :, :, k]
-        return remote(there, there, d_send.at[k], d_recv.at[k], seq, sib)
+        bytes_of(ring_bytes(stage, k), w_recv.at[stage, k])
+
+    def ring_bytes(stage, k):
+        pair = slice(0, 2)
+        if stage == 0:
+            return spot(k, every, 0, pair, 0)
+        if stage == 1:
+            return spot(k, every, 0, 0, 0)
+        return spot(k, every, pair if stage == 2 else 0, every, 0)
+
+    def core_copy(k, part):
+        there = (
+            ga.at[:, c, 0, 0:3, k],
+            ga.at[:, c, 0, 3, k],
+            ga.at[:, c, 1:4, :, k],
+        )[part]
+        return remote(there, there, d_send.at[k, part], d_recv.at[k, part], seq, sib)
 
     def pump(step, k):
         with scope(f"pump_{step}_{k}"):
@@ -250,16 +254,22 @@
                 s1_start(k)
             elif step == 1:
                 s1_wait(k)
-                ring_start(2 if k in WIDE else 0, k)
+                ring_start(0, k)
             elif step <= 4:
                 ring_wait(step - 2, k)
                 ring_start(step - 1, k)
             elif step == 5:
                 ring_wait(3, k)
                 if k < ATT:
-                    core_copy(k).start()
+                    core_copy(k, 0).start()
+            elif step == 6:
+                core_copy(k, 1).start()
+                core_copy(k, 2).start()
+            elif step == 7:
+                core_copy(k, 0).wait_recv()
             else:
-                core_copy(k).wait_recv()
+                core_copy(k, 1).wait_recv()
+                core_copy(k, 2).wait_recv()
 
     def ag_copy(slot, b, way):
         to = (jnp.minimum(zl + 1, 3) * 2 + c, jnp.maximum(zl - 1, 0) * 2 + c, sib)[way]
@@ -378,16 +388,19 @@
         lax.fori_loop(half * 4, half * 4 + 4, one_block, 0)
 
     def send_rows(source, target, send, recv, b):
-        def start(i, _):
-            to = lax.rem(seq + i, N_SEQ)
-
-            @pl.when((to // 16 == b) | (b < 0))
-            def _():
-                remote(source.at[to], target.at[seq], send, recv, to, me).start()
-
-            return 0
-
-        lax.fori_loop(1, N_SEQ, start, 0)
+        for other in (1, 0):
+
+            def start(i, _):
+                to_x, to_y = lax.rem(x + i // 4, 4), lax.rem(y + i, 4)
+                to = (to_x * 2 + lax.rem(zh + other, 2)) * 4 + to_y
+
+                @pl.when((to // 16 == b) | (b < 0))
+                def _():
+                    remote(source.at[to], target.at[seq], send, recv, to, me).start()
+
+                return 0
+
+            lax.fori_loop(1 - other, 16, start, 0)
 
     def take_rows(source, target, recv):
         target[seq] = source[seq]
@@ -395,7 +408,6 @@
 
     def finish(b):
         with scope(f"finish_{b}"):
-            bytes_of(heads.at[b, 0:7], h_recv.at[b])
             mixed = heads[b].reshape(D, 128).T
             out = dot(mixed, ga[:, :, 0, 0:3].reshape(D, D)).astype(BF16).astype(F32)
             rows = pl.ds(b * 128, 128)
@@ -410,7 +422,7 @@
             [ga[z, core, u // 4, u % 4].reshape(48, D) for u in range(first, first + 3)], axis=0
         )
 
-    def temporal(half):
+    def temporal():
         rows = rows_in[...].astype(F32).reshape(256, D).astype(BF16)
         same = lax.rem(lax.broadcasted_iota(jnp.int32, (256, 256), 0), 8) == lax.rem(
             lax.broadcasted_iota(jnp.int32, (256, 256), 1), 8
@@ -420,9 +432,11 @@
 
         def pair_of_heads(t):
             z, core = t // 2, lax.rem(t, 2)
-            queries = head_norm_rows(dot(att_rows(z, core, 3), rows, 1, 1), column)
+            table = jnp.concatenate([att_rows(z, core, 3), att_rows(z, core, 9)], axis=0)
+            both = dot(table, rows, 1, 1)
+            queries = head_norm_rows(both[:HW], column)
             keys = head_norm_lanes(dot(rows, att_rows(z, core, 6), 1, 1), row).astype(BF16)
-            values = dot(att_rows(z, core, 9), rows, 1, 1).astype(BF16)
+            values = both[HW:].astype(BF16)
             parts = []
             for head in range(2):
                 kept = queries[head * HD : (head + 1) * HD]
@@ -433,15 +447,13 @@
                 parts.append(mixed[head * HD : (head + 1) * HD])
             return jnp.concatenate(parts, axis=0).astype(BF16)
 
-        def two_pairs(i, _):
-            first, second = pair_of_heads(2 * i), pair_of_heads(2 * i + 1)
-            tt[2 * i] = first
-            tt[2 * i + 1] = second
+        def four_pairs(i, _):
+            done = [pair_of_heads(4 * i + j) for j in range(4)]
+            for j in range(4):
+                tt[4 * i + j] = done[j]
             return 0
 
-        lax.fori_loop(half * 2, half * 2 + 2, two_pairs, 0)
-        if half == 0:
-            return
+        lax.fori_loop(0, 2, four_pairs, 0)
         out = dot(tt[...].reshape(D, 256).T, ga[:, :, 3, 0:3].reshape(D, D))
         rows_out[...] = out.reshape(N_SEQ, 8, D).astype(BF16)
 
@@ -461,32 +473,34 @@
             nm[c, rows] = normed.astype(BF16)
 
     def mlp_round(k, which):
-        u = dot(nm[which], gm[:, 0:2, :, k].reshape(768, D), 1, 1)
+        u = dot(nm[which], gm[k][:, 0:2].reshape(32 * MLP_ROWS[k], D), 1, 1)
         h = 0.5 * u * (1.0 + jnp.tanh(math.sqrt(2.0 / math.pi) * (u + 0.044715 * (u * u * u))))
-        product = dot(h.astype(BF16), gm[:, 2:4, :, k].reshape(768, D))
+        product = dot(h.astype(BF16), gm[k][:, 2:4].reshape(32 * MLP_ROWS[k], D))
         return product if k == 0 else total[which] + product
 
+    near = zl + 1 - 2 * lax.rem(zl, 2)
+    middle = 2 - zl // 2
+    far = 3 - 3 * (zl // 2)
+    with scope("greet"):
+        pl.semaphore_wait(barrier, len(peers) + N_SEQ - 1)
+    pump(0, 0)
+    pump(0, 1)
+    loads[0].wait()
+    loads[1].wait()
     for b in range(2):
         rows = lat[pl.ds(b * 128, 128)].astype(F32)
         xs[me, b] = (layer_norm(rows) * (1.0 + mod[1, b : b + 1]) + mod[0, b : b + 1]).astype(BF16)
-    with scope("greet"):
-        pl.semaphore_wait(barrier, len(peers) + N_SEQ - 1)
-    near = zl + 1 - 2 * lax.rem(zl, 2)
-    middle = 2 - zl // 2
-    far = 3 - 3 * (zl // 2)
-    pump(0, 0)
-    pump(0, 1)
-    ag_step(0, 0)
-    ag_step(0, 1)
-    for b in range(2):
-        take_core(zl, b)
-        project(zl, b)
+        ag_step(0, b)
     pump(1, 0)
+    loads[2].wait()
+    take_core(zl, 0)
+    project(zl, 0)
     pump(1, 1)
+    take_core(zl, 1)
+    project(zl, 1)
     pump(2, 0)
     pump(2, 1)
     pump(3, 0)
-    pump(0, 2)
     ag_step(1, 0)
     pump(3, 1)
     take_core(near, 0)
@@ -494,61 +508,67 @@
     ag_step(1, 1)
     take_core(near, 1)
     project(near, 1)
-    pump(0, 3)
     ag_step(2, 0)
+    pump(0, 2)
     pump(4, 0)
     take_core(middle, 0)
     project(middle, 0)
-    pump(1, 2)
     ag_step(2, 1)
+    pump(0, 3)
+    pump(0, 4)
     take_core(middle, 1)
     project(middle, 1)
     pump(4, 1)
-    pump(1, 3)
-    pump(2, 2)
+    pump(1, 2)
     ag_step(3, 0)
     take_core(far, 0)
     pump(5, 0)
     project(far, 0)
     attend(0, 0)
+    pump(2, 2)
+    attend(0, 1)
+    ag_step(3, 1)
     pump(3, 2)
-    attend(0, 1)
-    pump(2, 3)
-    ag_step(3, 1)
     take_core(far, 1)
     pump(5, 1)
-    pump(0, 4)
+    pump(6, 0)
+    pump(6, 1)
     project(far, 1)
     attend(1, 0)
     attend(1, 1)
-    pump(4, 2)
-    pump(6, 0)
-    pump(6, 1)
+    pump(1, 3)
+    pump(1, 4)
+    pump(7, 0)
+    pump(7, 1)
+    with scope("take_heads"):
+        for b in range(2):
+            bytes_of(heads.at[b, 0:7], h_recv.at[b])
     finish(0)
     finish(1)
-    pump(1, 4)
+    pump(4, 2)
+    pump(2, 3)
+    pump(2, 4)
     pump(3, 3)
     with scope("take_1"):
         take_rows(nrm, rows_in, x_sem.at[1])
+    pump(8, 0)
+    pump(8, 1)
     with scope("temporal"):
-        temporal(0)
-    pump(2, 4)
-    with scope("temporal"):
-        temporal(1)
+        temporal()
     send_rows(rows_out, rows_back, x_sem.at[2], x_sem.at[3], -1)
     pump(3, 4)
     pump(4, 3)
-    pump(5, 2)
+    pump(4, 4)
     with scope("take_2"):
         take_rows(rows_out, rows_back, x_sem.at[3])
     with scope("entry"):
         mlp_entry()
         half_copy().start()
+    pump(5, 2)
     with scope("mlp"):
         total[c] = mlp_round(0, c)
         half_copy().wait_recv()
         total[1 - c] = mlp_round(0, 1 - c)
-    pump(4, 4)
     pump(5, 3)
     with scope("mlp"):
         total[c] = mlp_round(1, c)
@@ -575,10 +595,11 @@
             bytes_of(ot.at[b, 0:7], h_send.at[b])
         for k in range(ROUNDS):
             bytes_of(s1_bytes(k), s1_send.at[k])
-            for stage in range(2 if k in WIDE else 0, 4):
-                bytes_of(ring_bytes(stage), w_send.at[stage, k])
+            for stage in range(4):
+                bytes_of(ring_bytes(stage, k), w_send.at[stage, k])
             if k < ATT:
-                core_copy(k).wait_send()
+                for part in range(3):
+                    core_copy(k, part).wait_send()
 
 
 def body(
@@ -600,9 +621,13 @@
         block_kernel,
         name="block",
         out_shape=jax.ShapeDtypeStruct((256, D), BF16),
-        in_specs=[vmem] * 5 + [hbm] * 5,
+        in_specs=[hbm] * 2 + [vmem] * 2 + [hbm] * 6,
         out_specs=vmem,
         scratch_shapes=[
+            pltpu.VMEM((256, D), BF16),
+            pltpu.VMEM((9, 2, D), F32),
+            pltpu.VMEM((3, HW, D), BF16),
+            dma((3,)),
             pltpu.VMEM((N_TP, 2, 128, D), BF16),
             pltpu.VMEM((2, N_TP, 128, HW), BF16),
             pltpu.VMEM((2, N_TP, HW, 128), BF16),
@@ -610,7 +635,7 @@
             pltpu.VMEM((2, N_TP, HW, 128), BF16),
             pltpu.VMEM((2, N_TP, HW, 128), BF16),
             pltpu.VMEM((4, 2, 4, 4, ATT, 24, D), BF16),
-            pltpu.VMEM((4, 4, 4, ROUNDS - ATT, 24, D), BF16),
+            *[pltpu.VMEM((4, 4, 4, rows, D), BF16) for rows in MLP_ROWS],
             pltpu.VMEM((256, D), F32),
             pltpu.VMEM((N_SEQ, 8, D), BF16),
             pltpu.VMEM((N_SEQ, 8, D), BF16),
@@ -628,8 +653,8 @@
             dma((ROUNDS,)),
             dma((4, ROUNDS)),
             dma((4, ROUNDS)),
-            dma((ATT,)),
-            dma((ATT,)),
+            dma((ATT, 3)),
+            dma((ATT, 3)),
             dma((2,)),
             dma((2,)),
             dma((4,)),
@@ -648,8 +673,8 @@
         out_spatial.reshape(3, ATT, 24, D),
         qkv_temporal.transpose(0, 2, 1).reshape(9, ATT, 24, D),
         out_temporal.reshape(3, ATT, 24, D),
-        fc_in.T.reshape(2, 4, ROUNDS - ATT, 24, D),
-        fc_out.reshape(2, 4, ROUNDS - ATT, 24, D),
+        fc_in.T.reshape(2, 4, 72, D),
+        fc_out.reshape(2, 4, 72, D),
     )
     return result.reshape(latent.shape)
 

time: 142 us -> 138 us (0.972)
  the two profiles are of different devices: /device:TPU:121 before, /device:TPU:1 now
where the time goes in v5:
time: 138 us
  Pallas kernels  136 us (99%)
  local copies, waits for them, and re-layouts  1.92 us (1%)
    pallas_call x1, Pallas kernels, body(): pl.pallas_call(block_kernel, name='block', out_shape=jax.ShapeDtypeStruct...  136 us

profile of v5, /device:TPU:1, one launch (start us, length us, event | category | flops | bytes accessed | tf_op | source)
XLA Modules:
  0.0 138.2 jit_solution(17802485443750581413)
XLA Ops:
  0.0 136.3 %block.1 = bf16[256,1152]{1,0:T(8,128)(2,1)} custom-call(bf16[256,1152]{1,0:T(8,128)(2,1)} %bitcast.20, f32[9,2,1152]{2,1,0:T(2,128)} %bitcast.23, f32[2,72]{1,0:T(2,128)} %gain_s.1, f32[2,72]{1,0:T(2,128)} %gain_t.1, bf16[3,144,1152]{2,1,0:T(8,128)(2,1)} %bitcast.18, bf16[3,2,24,1152]{3,2,1,0:T(8,128)(2,1)} %bitcast.21, bf16[9,2,24,1152]{3,2,1,0:T(8,128)(2,1)} %bitcast.19, ...), custom_call_target="tpu_custom_call" | custom-call | tf_op jit(solution)/shard_map/block/pallas_call | solution.py:620
  136.3 1.9 %copy.13 = bf16[2,1,128,1152]{3,2,1,0:T(8,128)(2,1)} copy(bf16[2,1,128,1152]{3,2,1,0:T(8,128)(2,1)} %bitcast.15) | data formatting | bytes 1179648

commit v6 on v5

--- a/solution.py
+++ b/solution.py
@@ -620,7 +620,7 @@
     result = pl.pallas_call(
         block_kernel,
         name="block",
-        out_shape=jax.ShapeDtypeStruct((256, D), BF16),
+        out_shape=pltpu.VMEM((256, D), BF16),
         in_specs=[hbm] * 2 + [vmem] * 2 + [hbm] * 6,
         out_specs=vmem,
         scratch_shapes=[

time: 138 us -> 136 us (0.986)
  no operation moved by 1% of the time
where the time goes in v6:
time: 136 us
  Pallas kernels  135 us (99%)
    pallas_call x1, Pallas kernels, body(): pl.pallas_call(block_kernel, name='block', out_shape=pltpu.VMEM((256, D),...  135 us

profile of v6, /device:TPU:1, one launch (start us, length us, event | category | flops | bytes accessed | tf_op | source)
XLA Modules:
  0.0 136.3 jit_solution(4996739056604107825)
XLA Ops:
  0.0 135.5 %block.1 = bf16[256,1152]{1,0:T(8,128)(2,1)S(1)} custom-call(bf16[256,1152]{1,0:T(8,128)(2,1)} %bitcast.20, f32[9,2,1152]{2,1,0:T(2,128)} %bitcast.23, f32[2,72]{1,0:T(2,128)} %gain_s.1, f32[2,72]{1,0:T(2,128)} %gain_t.1, bf16[3,144,1152]{2,1,0:T(8,128)(2,1)} %bitcast.18, bf16[3,2,24,1152]{3,2,1,0:T(8,128)(2,1)} %bitcast.21, ...), custom_call_target="tpu_custom_call" | custom-call | tf_op jit(solution)/shard_map/block/pallas_call | solution.py:620
  135.5 0.8 copy.13

commit v7 on v6

--- a/solution.py
+++ b/solution.py
@@ -20,7 +20,7 @@
 BF16 = jnp.bfloat16
 
 ATT = 2
-MLP_ROWS = (32, 32, 8)
+MLP_ROWS = (32, 24, 16)
 ROUNDS = ATT + len(MLP_ROWS)
 
 

time: 136 us -> 135 us (level)
    pallas_call x1, Pallas kernels: 135 us -> 134 us  [body(): pl.pallas_call(block_kernel, name='block', out_shape=pltpu.VMEM((256, D),...]
where the time goes in v7:
time: 135 us; the launch traced here: 134 us
  Pallas kernels  134 us (99%)
    pallas_call x1, Pallas kernels, body(): pl.pallas_call(block_kernel, name='block', out_shape=pltpu.VMEM((256, D),...  134 us

profile of v7, /device:TPU:1, one launch (start us, length us, event | category | flops | bytes accessed | tf_op | source)
XLA Modules:
  0.0 134.5 jit_solution(13360028279027527054)
XLA Ops:
  0.0 133.6 %block.1 = bf16[256,1152]{1,0:T(8,128)(2,1)S(1)} custom-call(bf16[256,1152]{1,0:T(8,128)(2,1)} %bitcast.20, f32[9,2,1152]{2,1,0:T(2,128)} %bitcast.23, f32[2,72]{1,0:T(2,128)} %gain_s.1, f32[2,72]{1,0:T(2,128)} %gain_t.1, bf16[3,144,1152]{2,1,0:T(8,128)(2,1)} %bitcast.18, bf16[3,2,24,1152]{3,2,1,0:T(8,128)(2,1)} %bitcast.21, ...), custom_call_target="tpu_custom_call" | custom-call | tf_op jit(solution)/shard_map/block/pallas_call | solution.py:620
  133.6 0.8 copy.13
